TPU v7x, 32 devices: a 4x4x1 block of a 4x4x8 slice. The times are simulated.
32 devices in a mesh: dp: 1 (over z), my: 4 (over y), mx: 8 (over x, core).
Axes of the slice: x: 4, y: 4, z: 1, core: 2. Of those that a mesh axis runs over, the one named last changes fastest.
The devices are a block of a 4x4x8 slice.
Arguments:
- x_in: bfloat16 [4096, 7168], P('dp', 'my')
- gain_attn: bfloat16 [7168], P('my')
- w_q: bfloat16 [7168, 56, 128], P('my', 'mx')
- w_k: bfloat16 [7168, 8, 128], P('my', 'mx')
- w_v: bfloat16 [7168, 8, 128], P('my', 'mx')
- w_o: bfloat16 [56, 128, 7168], P('mx', None, 'my')
- gain_mlp: bfloat16 [7168], P('my')
- w_gate: bfloat16 [7168, 20480], P('my', 'mx')
- w_up: bfloat16 [7168, 20480], P('my', 'mx')
- w_down: bfloat16 [20480, 7168], P('mx', 'my')
Outputs:
- output: bfloat16 [4096, 7168], P('dp', 'my')
All inputs are finite; a program needn't handle non-finite values.
Results may differ from a plain program's by a relative error of at most 0.0138619.
Values are sent between devices in bfloat16 or wider.
A program may use at most 768 MiB of HBM per device.

v0:
```python
import jax
import jax.numpy as jnp
from jax import lax
from jax.sharding import PartitionSpec as P

ROPE_BASE = 10000.0
NORM_EPS = 1e-6


def apply_rope(values, positions):
    half_dim = values.shape[-1] // 2
    inv_freq = ROPE_BASE ** (-jnp.arange(half_dim, dtype=jnp.float32) / half_dim)
    angles = positions[:, None] * inv_freq[None, :]
    cos_t = jnp.cos(angles)[:, None, :]
    sin_t = jnp.sin(angles)[:, None, :]
    values_f = values.astype(jnp.float32)
    first_half = values_f[..., :half_dim]
    second_half = values_f[..., half_dim:]
    return jnp.concatenate([first_half * cos_t - second_half * sin_t, second_half * cos_t + first_half * sin_t], axis=-1).astype(jnp.bfloat16)


def attend_local(q_rot, k_full, v_full, query_pos):
    q_tokens, heads_loc, head_dim = q_rot.shape
    kv_loc = k_full.shape[1]
    q_grp = q_rot.reshape(q_tokens, kv_loc, heads_loc // kv_loc, head_dim)
    scores = jnp.einsum("qkgd,tkd->qkgt", q_grp, k_full, preferred_element_type=jnp.float32) * head_dim ** -0.5
    key_pos = jnp.arange(k_full.shape[0])
    causal = key_pos[None, :] <= query_pos[:, None]
    scores = jnp.where(causal[:, None, None, :], scores, -jnp.inf)
    attn_prob = jax.nn.softmax(scores, axis=-1).astype(jnp.bfloat16)
    attn_out = jnp.einsum("qkgt,tkd->qkgd", attn_prob, v_full, preferred_element_type=jnp.float32)
    return attn_out.astype(jnp.bfloat16).reshape(q_tokens, heads_loc, head_dim)


def solution(mesh):
    my_size = mesh.shape["my"]

    def width_norm(values, gain, width):
        values_f = values.astype(jnp.float32)
        row_sq = lax.psum(jnp.sum(values_f * values_f, axis=-1, keepdims=True), "my")
        return (values_f * lax.rsqrt(row_sq / width + NORM_EPS) * gain.astype(jnp.float32)).astype(jnp.bfloat16)

    def local_layer(x_in, gain_attn, w_q, w_k, w_v, w_o, gain_mlp, w_gate, w_up, w_down):
        tokens = x_in.shape[0]
        width = x_in.shape[1] * my_size
        q_tokens = tokens // my_size
        row_idx = lax.axis_index("my")
        normed = width_norm(x_in, gain_attn, width)
        q_part = jnp.einsum("td,dhe->the", normed, w_q, preferred_element_type=jnp.float32).astype(jnp.bfloat16)
        k_part = jnp.einsum("td,dhe->the", normed, w_k, preferred_element_type=jnp.float32).astype(jnp.bfloat16)
        v_part = jnp.einsum("td,dhe->the", normed, w_v, preferred_element_type=jnp.float32).astype(jnp.bfloat16)
        q_loc = lax.psum_scatter(q_part, "my", scatter_dimension=0, tiled=True)
        k_loc = lax.psum_scatter(k_part, "my", scatter_dimension=0, tiled=True)
        v_loc = lax.psum_scatter(v_part, "my", scatter_dimension=0, tiled=True)
        query_pos = row_idx * q_tokens + jnp.arange(q_tokens)
        q_rot = apply_rope(q_loc, query_pos.astype(jnp.float32))
        k_rot = apply_rope(k_loc, query_pos.astype(jnp.float32))
        k_full = lax.all_gather(k_rot, "my", axis=0, tiled=True)
        v_full = lax.all_gather(v_loc, "my", axis=0, tiled=True)
        attn_loc = attend_local(q_rot, k_full, v_full, query_pos)
        attn_all = lax.all_gather(attn_loc, "my", axis=0, tiled=True)
        attn_part = jnp.einsum("the,hed->td", attn_all, w_o, preferred_element_type=jnp.float32).astype(jnp.bfloat16)
        attn_sum = lax.psum(attn_part, "mx")
        residual = (x_in.astype(jnp.float32) + attn_sum.astype(jnp.float32)).astype(jnp.bfloat16)
        normed_mlp = width_norm(residual, gain_mlp, width)
        gate_part = jnp.dot(normed_mlp, w_gate, preferred_element_type=jnp.float32).astype(jnp.bfloat16)
        up_part = jnp.dot(normed_mlp, w_up, preferred_element_type=jnp.float32).astype(jnp.bfloat16)
        gate_sum = lax.psum(gate_part, "my")
        up_sum = lax.psum(up_part, "my")
        act_val = (jax.nn.silu(gate_sum.astype(jnp.float32)) * up_sum.astype(jnp.float32)).astype(jnp.bfloat16)
        down_part = jnp.dot(act_val, w_down, preferred_element_type=jnp.float32).astype(jnp.bfloat16)
        down_sum = lax.psum(down_part, "mx")
        return (residual.astype(jnp.float32) + down_sum.astype(jnp.float32)).astype(jnp.bfloat16)

    in_specs = (P("dp", "my"), P("my"), P("my", "mx", None), P("my", "mx", None), P("my", "mx", None), P("mx", None, "my"), P("my"), P("my", "mx"), P("my", "mx"), P("mx", "my"))
    return jax.shard_map(local_layer, mesh=mesh, in_specs=in_specs, out_specs=P("dp", "my"), check_vma=False)
```

profile of v0, /device:TPU:97, one launch (start us, length us, event | category | flops | bytes accessed | tf_op | source)
XLA Modules:
  0.0 1621.5 jit_solution(7224883797181551487)
XLA Ops:
  6.6 8.3 fusion.9
  14.8 15.9 psum.42
  30.8 8.9 fusion.29
  39.8 8.3 fusion.28
  48.7 21.7 %fusion.25 = bf16[4096,7,128]{2,0,1:T(8,128)(2,1)} fusion(bf16[1792,7,128]{2,0,1:T(8,128)(2,1)} %param.12, bf16[4096,1792]{1,0:T(8,128)(2,1)} %param.10, f32[1792]{0:T(1024)S(1)} %convert_element_type.107, f32[4096]{0:T(1024)S(1)} %bitcast.71), kind=kOutput, calls=%fused_computation.37 | convolution fusion | flops 13186367488 | bytes 25254912 | tf_op jit(solution)/shard_map/td,dhe->the/dot_general | solution.py:49
  76.7 5.7 iota_compare_fusion
  82.4 3.3 reduce-scatter.4.cloned.1.call-done
  85.8 73.6 %reduce-scatter.8.cloned.1.call-done = bf16[1024,7,128]{2,0,1:T(8,128)(2,1)} async-done(((bf16[4096,7,128]{2,0,1:T(8,128)(2,1)}), bf16[1024,7,128]{2,0,1:T(8,128)(2,1)}) %reduce-scatter.8.cloned.1.call-update) | async-done | bytes 1835024 | tf_op jit(solution)/shard_map/reduce_scatter | solution.py:52
  161.1 4.3 subtract_convert_fusion
  165.4 14.6 all-gather.7.cloned.1.call-done
  179.9 44.0 %fusion.1 = (f32[1024,7]{0,1:T(8,128)S(1)}, f32[4096,1024,7]{1,0,2:T(8,128)}) fusion(pred[1024,4096]{0,1:T(8,128)(4,1)} %iota_compare_fusion, bf16[1024,7,64]{2,0,1:T(8,128)(2,1)} %get-tuple-element.10, bf16[1024,7,64]{2,0,1:T(8,128)(2,1)} %get-tuple-element.9, bf16[4096,1,128]{0,2,1:T(8,128)(2,1)} %all-gather.7.cloned.1.call-done), kind=kOutput, calls=%fused_computation.4 | convolution fusion | flops 7607936000 | bytes 124547072 | tf_op jit(solution)/shard_map/qkgd,tkd->qkgt/dot_general | solution.py:26
  224.0 37.5 %fusion = f32[1024,7]{0,1:T(8,128)S(1)} fusion(f32[4096,1024,7]{1,0,2:T(8,128)} %get-tuple-element.16, f32[1024,7]{0,1:T(8,128)S(1)} %get-tuple-element.15, pred[1024,4096]{0,1:T(8,128)(4,1)} %iota_compare_fusion), kind=kLoop, calls=%fused_computation.3 | loop fusion | flops 117433344 | bytes 121692160 | tf_op jit(solution)/shard_map/reduce_sum | solution.py:30
  261.5 46.8 %convert_bitcast_fusion = bf16[1024,1,7,128]{0,3,2,1:T(8,128)(2,1)} fusion(f32[1024,7]{0,1:T(8,128)S(1)} %fusion, f32[1024,7]{0,1:T(8,128)S(1)} %get-tuple-element.15, f32[4096,1024,7]{1,0,2:T(8,128)} %get-tuple-element.16, pred[1024,4096]{0,1:T(8,128)(4,1)} %iota_compare_fusion, bf16[4096,1,128]{2,0,1:T(8,128)(2,1)} %all-gather.5.cloned.1.call-done), kind=kOutput, calls=%fused_computation.48 | convolution fusion | flops 7663910912 | bytes 124575744 | tf_op jit(solution)/shard_map/qkgt,tkd->qkgd/dot_general | solution.py:31
  308.4 74.5 %all-gather.9.cloned.1.call-done = bf16[4096,1,7,128]{0,3,2,1:T(8,128)(2,1)} async-done(((bf16[1024,1,7,128]{0,3,2,1:T(8,128)(2,1)}), bf16[4096,1,7,128]{0,3,2,1:T(8,128)(2,1)}) %all-gather.9.cloned.1.call-update) | async-done | bytes 7340048 | tf_op jit(solution)/shard_map/all_gather | solution.py:61
  382.9 21.7 %bitcast_convert_fusion = bf16[4096,1792]{1,0:T(8,128)(2,1)} fusion(bf16[7,128,1792]{2,1,0:T(8,128)(2,1)S(1)} %copy-done, bf16[4096,1,7,128]{0,3,2,1:T(8,128)(2,1)} %all-gather.9.cloned.1.call-done), kind=kOutput, calls=%fused_computation.28 | convolution fusion | flops 13160677376 | bytes 25231360 | tf_op jit(solution)/shard_map/the,hed->td/dot_general | solution.py:62
  405.3 158.7 %all-reduce.5.cloned.1.call-done = bf16[4096,1792]{1,0:T(8,128)(2,1)} async-done(((bf16[4096,1792]{1,0:T(8,128)(2,1)}), bf16[4096,1792]{1,0:T(8,128)(2,1)}) %all-reduce.5.cloned.1.call-update) | async-done | bytes 14680080 | tf_op jit(solution)/shard_map/psum | solution.py:63
  564.0 18.2 %fusion.13 = (f32[4096]{0:T(1024)S(1)}, bf16[4096,1792]{1,0:T(8,128)(2,1)}) fusion(bf16[4096,1792]{1,0:T(8,128)(2,1)} %all-reduce.5.cloned.1.call-done, bf16[4096,1792]{1,0:T(8,128)(2,1)} %param.10), kind=kLoop, calls=%fused_computation.24 | loop fusion | flops 51376128 | bytes 44056576 | tf_op jit(solution)/shard_map/reduce_sum | solution.py:40
  582.2 13.2 psum.44
  595.4 46.0 %convolution_convert_fusion.1 = bf16[4096,2560]{1,0:T(8,128)(2,1)} fusion(bf16[1792,2560]{1,0:T(8,128)(2,1)} %param.17, bf16[4096,1792]{1,0:T(8,128)(2,1)} %get-tuple-element.8, f32[1792]{0:T(1024)S(1)} %convert_element_type.125, f32[4096]{0:T(1024)S(1)} %bitcast.72), kind=kOutput, calls=%fused_computation.30 | convolution fusion | flops 37620809728 | bytes 44850176 | tf_op jit(solution)/shard_map/dot_general | solution.py:66
  641.4 46.3 %convolution_convert_fusion = bf16[4096,2560]{1,0:T(8,128)(2,1)} fusion(bf16[1792,2560]{1,0:T(8,128)(2,1)} %param.18, bf16[4096,1792]{1,0:T(8,128)(2,1)S(1)} %copy-done.2, f32[1792]{0:T(1024)S(1)} %convert_element_type.125, f32[4096]{0:T(1024)S(1)} %bitcast.73), kind=kOutput, calls=%fused_computation.29 | convolution fusion | flops 37620809728 | bytes 44850176 | tf_op jit(solution)/shard_map/dot_general | solution.py:67
  687.8 696.1 %all-reduce.9.cloned.1.call-done = (bf16[4096,2560]{1,0:T(8,128)(2,1)}, bf16[4096,2560]{1,0:T(8,128)(2,1)}) async-done(((bf16[4096,2560]{1,0:T(8,128)(2,1)}, bf16[4096,2560]{1,0:T(8,128)(2,1)}), (bf16[4096,2560]{1,0:T(8,128)(2,1)}, bf16[4096,2560]{1,0:T(8,128)(2,1)})) %all-reduce.9.cloned.1.call-update) | async-done | bytes 41943056 | tf_op jit(solution)/shard_map/psum | solution.py:69
  1383.9 54.1 %fusion.19 = bf16[4096,1792]{1,0:T(8,128)(2,1)} fusion(bf16[2560,1792]{1,0:T(8,128)(2,1)} %param.19, bf16[4096,2560]{1,0:T(8,128)(2,1)} %get-tuple-element.5, bf16[4096,2560]{1,0:T(8,128)(2,1)} %get-tuple-element.6), kind=kOutput, calls=%fused_computation.33 | convolution fusion | flops 37672189952 | bytes 65798144 | tf_op jit(solution)/shard_map/dot_general | solution.py:71
  1438.1 159.0 %all-reduce.7.cloned.1.call-done = bf16[4096,1792]{1,0:T(8,128)(2,1)} async-done(((bf16[4096,1792]{1,0:T(8,128)(2,1)}), bf16[4096,1792]{1,0:T(8,128)(2,1)}) %all-reduce.7.cloned.1.call-update) | async-done | bytes 14680080 | tf_op jit(solution)/shard_map/psum | solution.py:72
  1597.1 17.4 %fusion.16 = bf16[4096,1792]{1,0:T(8,128)(2,1)} fusion(bf16[4096,1792]{1,0:T(8,128)(2,1)} %get-tuple-element.8, bf16[4096,1792]{1,0:T(8,128)(2,1)} %all-reduce.7.cloned.1.call-done), kind=kLoop, calls=%fused_computation.27 | loop fusion | flops 29360128 | bytes 44040192 | tf_op jit(solution)/shard_map/convert_element_type | solution.py:73
  (42 shorter events, 9.8 us)
Async XLA Ops:
  6.5 376.3 %copy-start = (bf16[7,128,1792]{2,1,0:T(8,128)(2,1)S(1)}, bf16[7,128,1792]{2,1,0:T(8,128)(2,1)}, u32[]{:S(2)}) copy-start(bf16[7,128,1792]{2,1,0:T(8,128)(2,1)} %param.15) | copy-start | bytes 9633796
  6.6 24.2 %copy-start.3 = (bf16[1792]{0:T(1024)(128)(2,1)S(1)}, bf16[1792]{0:T(1024)(128)(2,1)}, u32[]{:S(2)}) copy-start(bf16[1792]{0:T(1024)(128)(2,1)} %param.11) | copy-start | bytes 10756
  6.6 64.0 %reduce-scatter.6.cloned.1.call-start = ((), (), s32[]{:S(2)}) async-start(), calls=%async_computation.5 | async-start | bytes 1310720 | tf_op jit(solution)/shard_map/reduce_scatter | solution.py:53
  39.7 46.0 %reduce-scatter.4.cloned.1.call-start = ((), (), s32[]{:S(2)}) async-start(), calls=%async_computation.3 | async-start | bytes 1310720 | tf_op jit(solution)/shard_map/reduce_scatter | solution.py:54
  48.1 111.3 %reduce-scatter.8.cloned.1.call-start = ((), (), s32[]{:S(2)}) async-start(), calls=%async_computation.7 | async-start | bytes 9175040 | tf_op jit(solution)/shard_map/reduce_scatter | solution.py:52
  70.4 109.5 %all-gather.7.cloned.1.call-start = ((), (), s32[]{:S(2)}) async-start(), calls=%async_computation.6 | async-start | bytes 1310720 | tf_op jit(solution)/shard_map/all_gather | solution.py:58
  73.5 188.0 %all-gather.5.cloned.1.call-start = ((), (), s32[]{:S(2)}) async-start(), calls=%async_computation.4 | async-start | bytes 1310720 | tf_op jit(solution)/shard_map/all_gather | solution.py:59
  85.8 297.1 %all-gather.9.cloned.1.call-start = ((), (), s32[]{:S(2)}) async-start(), calls=%async_computation.10 | async-start | bytes 9175040 | tf_op jit(solution)/shard_map/all_gather | solution.py:61
  308.3 255.7 %all-reduce.5.cloned.1.call-start = ((), (), s32[]{:S(2)}) async-start(), calls=%async_computation.8 | async-start | bytes 29360128 | tf_op jit(solution)/shard_map/psum | solution.py:63
  404.6 0.7 copy-start.4
  404.7 979.3 %all-reduce.9.cloned.1.call-start = ((), (), s32[]{:S(2)}) async-start(), calls=%async_computation.11 | async-start | bytes 83886080 | tf_op jit(solution)/shard_map/psum | solution.py:69
  595.4 46.0 %copy-start.2 = (bf16[4096,1792]{1,0:T(8,128)(2,1)S(1)}, bf16[4096,1792]{1,0:T(8,128)(2,1)}, u32[]{:S(2)}) copy-start(bf16[4096,1792]{1,0:T(8,128)(2,1)} %get-tuple-element.8) | copy-start | bytes 44040196
  687.8 909.4 %all-reduce.7.cloned.1.call-start = ((), (), s32[]{:S(2)}) async-start(), calls=%async_computation.9 | async-start | bytes 29360128 | tf_op jit(solution)/shard_map/psum | solution.py:72
  1438.1 176.4 %copy-start.1 = (bf16[7,128,1792]{2,1,0:T(8,128)(2,1)S(1)}, bf16[7,128,1792]{2,1,0:T(8,128)(2,1)}, u32[]{:S(2)}) copy-start(bf16[7,128,1792]{2,1,0:T(8,128)(2,1)} %param.15) | copy-start | bytes 9633796
Sparse Core Ops, SparseCore 0:
  39.8 22.5 reduce-scatter.5
  64.7 20.9 reduce-scatter.3
  88.0 71.3 reduce-scatter.7
  160.8 19.0 all-gather.6
  181.4 21.8 all-gather.4
  308.4 74.3 all-gather.8
  404.8 159.1 all-reduce.4
  687.9 696.0 all-reduce.8
  1438.2 158.8 all-reduce.6
where the time goes:
time: 1630 us; the launch traced here: 1620 us
  waiting for transfers between devices  1180 us (72%)
  matrix products  298 us (18%)
  other arithmetic  99 us (6%)
  blocking collectives  29.1 us (2%)
    psum x1, waiting for transfers between devices, local_layer(): up_sum = lax.psum(up_part, 'my')  696 us
    psum x1, waiting for transfers between devices, local_layer(): down_sum = lax.psum(down_part, 'mx')  159 us
    psum x1, waiting for transfers between devices, local_layer(): attn_sum = lax.psum(attn_part, 'mx')  159 us
    all_gather x1, waiting for transfers between devices, local_layer(): attn_all = lax.all_gather(attn_loc, 'my', axis=0, tiled=True)  74.5 us
    reduce_scatter x1, waiting for transfers between devices, local_layer(): q_loc = lax.psum_scatter(q_part, 'my', scatter_dimension=0, tiled=True)  73.6 us
    dot_general x1, matrix products, local_layer(): jnp.dot(act_val, w_down, preferred_element_type=jnp.float32)  54.1 us
    dot_general x1, matrix products, attend_local(): jnp.einsum('qkgt,tkd->qkgd', attn_prob, v_full, preferred_element_type=jn...  46.8 us
    dot_general x1, matrix products, local_layer(): jnp.dot(normed_mlp, w_up, preferred_element_type=jnp.float32)  46.3 us
  transfers between devices with their start and end apart: 9, of which 7 were waited for; matrix products, arithmetic and copies ran while one was open for 8% of the time, Pallas kernels for 0%

commit v1 on v0

--- a/solution.py
+++ b/solution.py
@@ -1,10 +1,18 @@
+import functools
+
 import jax
 import jax.numpy as jnp
 from jax import lax
+from jax.experimental import pallas as pl
+from jax.experimental.pallas import tpu as pltpu
 from jax.sharding import PartitionSpec as P
 
 ROPE_BASE = 10000.0
 NORM_EPS = 1e-6
+CHUNK = 512
+MESH = pl.DeviceIdType.MESH
+F32 = jnp.float32
+BF16 = jnp.bfloat16
 
 
 def apply_rope(values, positions):
@@ -32,7 +40,323 @@
     return attn_out.astype(jnp.bfloat16).reshape(q_tokens, heads_loc, head_dim)
 
 
-def solution(mesh):
+class Place:
+    def __init__(self):
+        self.y = lax.axis_index("my")
+        mx = lax.axis_index("mx")
+        self.x = mx // 2
+        self.core = mx % 2
+        self.yp = (self.y + 1) % 4
+        self.ym = (self.y + 3) % 4
+        self.yo = (self.y + 2) % 4
+        self.xp = (self.x + 1) % 4
+        self.xm = (self.x + 3) % 4
+        self.xo = (self.x + 2) % 4
+        self.dev_yp = {"my": self.yp}
+        self.dev_ym = {"my": self.ym}
+        self.dev_xp = {"mx": self.xp * 2 + self.core}
+        self.dev_xm = {"mx": self.xm * 2 + self.core}
+        self.dev_core = {"mx": self.x * 2 + (1 - self.core)}
+        self.partners = (self.dev_yp, self.dev_ym, self.dev_xp, self.dev_xm, self.dev_core)
+
+    def entry(self):
+        barrier = pltpu.get_barrier_semaphore()
+        for dev in self.partners:
+            pl.semaphore_signal(barrier, inc=1, device_id=dev, device_id_type=MESH)
+        pl.semaphore_wait(barrier, len(self.partners))
+
+    def give_credit(self, credit):
+        for slot, dev in ((1, self.dev_yp), (0, self.dev_ym), (3, self.dev_xp), (2, self.dev_xm), (4, self.dev_core)):
+            pl.semaphore_signal(credit.at[slot], inc=1, device_id=dev, device_id_type=MESH)
+
+    def take_credit(self, credit):
+        for slot in range(5):
+            pl.semaphore_wait(credit.at[slot], 1)
+
+
+def rcopy(src, dst, send_sem, recv_sem, dev):
+    return pltpu.make_async_remote_copy(src_ref=src, dst_ref=dst, send_sem=send_sem, recv_sem=recv_sem, device_id=dev, device_id_type=MESH)
+
+
+def rows(start, size, align):
+    return pl.ds(pl.multiple_of(start, align), size)
+
+
+def mlp_kernel(n_chunks, m_hbm, h_hbm, wg_hbm, wu_hbm, wd_hbm, y_hbm, WG, WU, WD, M, PP, R1, R2, ACT, DP, DR, XR1, XR2, YB, H,
+               w_sem, m_sem, h_sem, y_sem, credit, s1s, s1r, s2s, s2r, acs, acr, fws, fwr, dds, ddr, x1s, x1r, x2s, x2r, xas, xar, xfs, xfr, dys, dyr):
+    at = Place()
+    tc, width = M.shape
+    ff = WG.shape[1]
+    qb = tc // 4
+    hq = qb // 2
+    hb = tc // 2
+    xb = hb // 4
+    hx = xb // 2
+    gu_tiles = 5
+    gu_w = ff // gu_tiles
+    dn_w = 256 if width % 256 == 0 else 128
+
+    w_copies = [pltpu.make_async_copy(s, d, w_sem.at[i]) for i, (s, d) in enumerate(((wg_hbm, WG), (wu_hbm, WU), (wd_hbm, WD)))]
+    for c in w_copies:
+        c.start()
+
+    def m_copy(c):
+        return pltpu.make_async_copy(m_hbm.at[rows(c * tc, tc, tc)], M, m_sem)
+
+    m_copy(0).start()
+    at.entry()
+
+    def gu_part(par, lo, hi):
+        @pl.loop(lo, hi)
+        def _(n):
+            g_cols = rows(n * gu_w, gu_w, 128)
+            PP[par, :, g_cols] = jnp.dot(M[...], WG[:, g_cols], preferred_element_type=F32).astype(BF16)
+            PP[par, :, rows(ff + n * gu_w, gu_w, 128)] = jnp.dot(M[...], WU[:, g_cols], preferred_element_type=F32).astype(BF16)
+
+    def s1_copies(par):
+        o = at.yo * qb
+        return (rcopy(PP.at[par, rows(o, hq, hq)], R1.at[0], s1s.at[0], s1r.at[0], at.dev_yp),
+                rcopy(PP.at[par, rows(o + hq, hq, hq)], R1.at[1], s1s.at[1], s1r.at[1], at.dev_ym))
+
+    def s2_copies(par):
+        return (rcopy(PP.at[par, rows(at.yp * qb, qb, qb)], R2.at[par, 0], s2s.at[par, 0], s2r.at[par, 0], at.dev_yp),
+                rcopy(PP.at[par, rows(at.ym * qb, qb, qb)], R2.at[par, 1], s2s.at[par, 1], s2r.at[par, 1], at.dev_ym))
+
+    def act_copies(par):
+        own = ACT.at[par, rows(at.y * qb, qb, qb)]
+        return (rcopy(own, own, acs.at[0], acr.at[0], at.dev_yp), rcopy(own, own, acs.at[1], acr.at[1], at.dev_ym))
+
+    def fwd_copies(par):
+        a = ACT.at[par, rows(at.ym * qb, hq, hq)]
+        b = ACT.at[par, rows(at.yp * qb + hq, hq, hq)]
+        return (rcopy(a, a, fws.at[par, 0], fwr.at[par, 0], at.dev_yp), rcopy(b, b, fws.at[par, 1], fwr.at[par, 1], at.dev_ym))
+
+    def dd_copy():
+        return rcopy(DP.at[rows((1 - at.core) * hb, hb, hb)], DR, dds, ddr, at.dev_core)
+
+    own_half = at.core * hb
+
+    def x1_copies():
+        o = own_half + at.xo * xb
+        return (rcopy(DP.at[rows(o, hx, hx)], XR1.at[0], x1s.at[0], x1r.at[0], at.dev_xp),
+                rcopy(DP.at[rows(o + hx, hx, hx)], XR1.at[1], x1s.at[1], x1r.at[1], at.dev_xm))
+
+    def x2_copies():
+        return (rcopy(DP.at[rows(own_half + at.xp * xb, xb, xb)], XR2.at[0], x2s.at[0], x2r.at[0], at.dev_xp),
+                rcopy(DP.at[rows(own_half + at.xm * xb, xb, xb)], XR2.at[1], x2s.at[1], x2r.at[1], at.dev_xm))
+
+    def yblk(b):
+        return YB.at[rows(own_half + b * xb, xb, xb)]
+
+    def xa_copies():
+        own = yblk(at.x)
+        return (rcopy(own, own, xas.at[0], xar.at[0], at.dev_xp), rcopy(own, own, xas.at[1], xar.at[1], at.dev_xm))
+
+    def xf_copies():
+        a = YB.at[rows(own_half + at.xm * xb, hx, hx)]
+        b = YB.at[rows(own_half + at.xp * xb + hx, hx, hx)]
+        return (rcopy(a, a, xfs.at[0], xfr.at[0], at.dev_xp), rcopy(b, b, xfs.at[1], xfr.at[1], at.dev_xm))
+
+    def dy_copy(i):
+        b = (at.x, at.xm, at.xp, at.xo)[i]
+        return rcopy(yblk(b), yblk(b), dys.at[i], dyr.at[i], at.dev_core)
+
+    def dy_wait_recv(i):
+        b = (at.x, at.xm, at.xp, at.xo)[i]
+        other = YB.at[rows((1 - at.core) * hb + b * xb, xb, xb)]
+        rcopy(other, other, dys.at[i], dyr.at[i], at.dev_core).wait_recv()
+
+    def h_copy(c):
+        return pltpu.make_async_copy(h_hbm.at[rows(c * tc + own_half + at.x * xb, xb, xb)], H, h_sem)
+
+    def y_copy(c):
+        return pltpu.make_async_copy(YB, y_hbm.at[rows(c * tc, tc, tc)], y_sem)
+
+    def start(copies):
+        for c in copies:
+            c.start()
+
+    def wait(copies):
+        for c in copies:
+            c.wait()
+
+    w_copies[0].wait()
+    w_copies[1].wait()
+    m_copy(0).wait()
+    gu_part(0, 0, gu_tiles)
+    w_copies[2].wait()
+
+    @pl.loop(0, n_chunks + 2)
+    def _(k):
+        par = k % 2
+        alt = (k + 1) % 2
+        has_s = k < n_chunks
+        has_gu = k + 1 < n_chunks
+        has_a = jnp.logical_and(k >= 1, k - 1 < n_chunks)
+        has_d = k >= 2
+
+        @pl.when(k >= 1)
+        def _():
+            at.take_credit(credit)
+
+        @pl.when(has_s)
+        def _():
+            start(s1_copies(par))
+
+        @pl.when(has_gu)
+        def _():
+            m_copy(k + 1).start()
+
+        @pl.when(has_d)
+        def _():
+            h_copy(k - 2).start()
+
+        @pl.when(has_a)
+        def _():
+            wait(s2_copies(alt))
+            base = at.y * qb
+            step = 16
+
+            @pl.loop(0, qb // step)
+            def _(i):
+                r = rows(base + i * step, step, step)
+                r2 = rows(i * step, step, step)
+                g = PP[alt, r, 0:ff].astype(F32) + R2[alt, 0, r2, 0:ff].astype(F32) + R2[alt, 1, r2, 0:ff].astype(F32)
+                u = PP[alt, r, ff:2 * ff].astype(F32) + R2[alt, 0, r2, ff:2 * ff].astype(F32) + R2[alt, 1, r2, ff:2 * ff].astype(F32)
+                ACT[alt, r, :] = (g * jax.nn.sigmoid(g) * u).astype(BF16)
+
+            start(act_copies(alt))
+
+        @pl.when(has_d)
+        def _():
+            wait(fwd_copies(par))
+
+            @pl.loop(0, width // dn_w)
+            def _(n):
+                cols = rows(n * dn_w, dn_w, 128)
+                DP[:, cols] = jnp.dot(ACT[par], WD[:, cols], preferred_element_type=F32).astype(BF16)
+
+            dd_copy().start()
+
+        @pl.when(has_s)
+        def _():
+            wait(s1_copies(par))
+            step = 16
+
+            @pl.loop(0, hq // step)
+            def _(i):
+                ri = rows(i * step, step, step)
+                ra = rows(at.yp * qb + i * step, step, step)
+                rb = rows(at.ym * qb + hq + i * step, step, step)
+                PP[par, ra, :] = (PP[par, ra, :].astype(F32) + R1[0, ri, :].astype(F32)).astype(BF16)
+                PP[par, rb, :] = (PP[par, rb, :].astype(F32) + R1[1, ri, :].astype(F32)).astype(BF16)
+
+            start(s2_copies(par))
+
+        @pl.when(has_d)
+        def _():
+            dd_copy().wait()
+            step = 16
+
+            @pl.loop(0, hb // step)
+            def _(i):
+                ri = rows(i * step, step, step)
+                ra = rows(own_half + i * step, step, step)
+                DP[ra, :] = (DP[ra, :].astype(F32) + DR[ri, :].astype(F32)).astype(BF16)
+
+            start(x1_copies())
+
+        @pl.when(has_gu)
+        def _():
+            m_copy(k + 1).wait()
+            gu_part(alt, 0, 2)
+
+        @pl.when(has_d)
+        def _():
+            wait(x1_copies())
+            ra = rows(own_half + at.xp * xb, hx, hx)
+            rb = rows(own_half + at.xm * xb + hx, hx, hx)
+            DP[ra, :] = (DP[ra, :].astype(F32) + XR1[0].astype(F32)).astype(BF16)
+            DP[rb, :] = (DP[rb, :].astype(F32) + XR1[1].astype(F32)).astype(BF16)
+            start(x2_copies())
+
+        @pl.when(has_gu)
+        def _():
+            gu_part(alt, 2, 3)
+
+        @pl.when(has_a)
+        def _():
+            wait(act_copies(alt))
+            start(fwd_copies(alt))
+
+        @pl.when(has_d)
+        def _():
+            wait(x2_copies())
+            h_copy(k - 2).wait()
+            r = rows(own_half + at.x * xb, xb, xb)
+            down = DP[r, :].astype(F32) + XR2[0].astype(F32) + XR2[1].astype(F32)
+            YB[r, :] = (H[...].astype(F32) + down).astype(BF16)
+            start(xa_copies())
+            dy_copy(0).start()
+
+        @pl.when(has_gu)
+        def _():
+            gu_part(alt, 3, 4)
+
+        @pl.when(has_d)
+        def _():
+            wait(xa_copies())
+            start(xf_copies())
+            dy_copy(1).start()
+            dy_copy(2).start()
+
+        @pl.when(has_gu)
+        def _():
+            gu_part(alt, 4, 5)
+
+        @pl.when(has_d)
+        def _():
+            wait(xf_copies())
+            dy_copy(3).start()
+            for i in range(4):
+                dy_copy(i).wait_send()
+                dy_wait_recv(i)
+            y_copy(k - 2).start()
+            y_copy(k - 2).wait()
+
+        @pl.when(k < n_chunks + 1)
+        def _():
+            at.give_credit(credit)
+
+
+def mlp_phase(m_full, h_full, w_gate, w_up, w_down, chunk):
+    tokens, width = m_full.shape
+    ff = w_gate.shape[1]
+    n_chunks = tokens // chunk
+    qb, hb = chunk // 4, chunk // 2
+    xb = hb // 4
+    hbm = pl.BlockSpec(memory_space=pl.ANY)
+    sem = pltpu.SemaphoreType.DMA
+    vm = lambda *s: pltpu.VMEM(s, BF16)
+    return pl.pallas_call(
+        functools.partial(mlp_kernel, n_chunks),
+        out_shape=jax.ShapeDtypeStruct((tokens, width), BF16),
+        in_specs=[hbm] * 5,
+        out_specs=hbm,
+        scratch_shapes=[
+            vm(width, ff), vm(width, ff), vm(ff, width), vm(chunk, width), vm(2, chunk, 2 * ff),
+            vm(2, qb // 2, 2 * ff), vm(2, 2, qb, 2 * ff), vm(2, chunk, ff), vm(chunk, width), vm(hb, width),
+            vm(2, xb // 2, width), vm(2, xb, width), vm(chunk, width), vm(xb, width),
+            sem((3,)), sem, sem, sem, pltpu.SemaphoreType.REGULAR((5,)),
+            sem((2,)), sem((2,)), sem((2, 2)), sem((2, 2)), sem((2,)), sem((2,)), sem((2, 2)), sem((2, 2)),
+            sem, sem, sem((2,)), sem((2,)), sem((2,)), sem((2,)), sem((2,)), sem((2,)), sem((2,)), sem((2,)), sem((4,)), sem((4,)),
+        ],
+        compiler_params=pltpu.CompilerParams(collective_id=1, has_side_effects=True, vmem_limit_bytes=67043328),
+        name="mlp_phase",
+    )(m_full, h_full, w_gate, w_up, w_down)
+
+
+def solution(mesh, chunk=CHUNK):
     my_size = mesh.shape["my"]
 
     def width_norm(values, gain, width):
@@ -63,14 +387,7 @@
         attn_sum = lax.psum(attn_part, "mx")
         residual = (x_in.astype(jnp.float32) + attn_sum.astype(jnp.float32)).astype(jnp.bfloat16)
         normed_mlp = width_norm(residual, gain_mlp, width)
-        gate_part = jnp.dot(normed_mlp, w_gate, preferred_element_type=jnp.float32).astype(jnp.bfloat16)
-        up_part = jnp.dot(normed_mlp, w_up, preferred_element_type=jnp.float32).astype(jnp.bfloat16)
-        gate_sum = lax.psum(gate_part, "my")
-        up_sum = lax.psum(up_part, "my")
-        act_val = (jax.nn.silu(gate_sum.astype(jnp.float32)) * up_sum.astype(jnp.float32)).astype(jnp.bfloat16)
-        down_part = jnp.dot(act_val, w_down, preferred_element_type=jnp.float32).astype(jnp.bfloat16)
-        down_sum = lax.psum(down_part, "mx")
-        return (residual.astype(jnp.float32) + down_sum.astype(jnp.float32)).astype(jnp.bfloat16)
+        return mlp_phase(normed_mlp, residual, w_gate, w_up, w_down, chunk)
 
     in_specs = (P("dp", "my"), P("my"), P("my", "mx", None), P("my", "mx", None), P("my", "mx", None), P("mx", None, "my"), P("my"), P("my", "mx"), P("my", "mx"), P("mx", "my"))
     return jax.shard_map(local_layer, mesh=mesh, in_specs=in_specs, out_specs=P("dp", "my"), check_vma=False)

time: 1630 us -> 1220 us (0.75)
  waiting for transfers between devices: 1180 us -> 329 us
  Pallas kernels: 0 us -> 584 us
  matrix products: 298 us -> 150 us
    psum x2 -> x0, waiting for transfers between devices: 855 us -> none  [the longest x1 696 us: local_layer(): up_sum = lax.psum(up_part, 'my')]
    pallas_call x0 -> x1, Pallas kernels: none -> 584 us  [mlp_phase(): pl.pallas_call(functools.partial(mlp_kernel, n_chunks), out_shape=jax.Sha...]
    dot_general x3 -> x0, matrix products: 146 us -> none  [the longest x1 54.1 us: local_layer(): jnp.dot(act_val, w_down, preferred_element_type=jnp.float32)]
  transfers between devices with their start and end apart: 9 -> 7, of which waited for: 7 -> 5; matrix products, arithmetic and copies ran while one was open for 8% -> 10% of each run, Pallas kernels for 0% -> 0%
where the time goes in v1:
time: 1220 us; the launch traced here: 1210 us
  Pallas kernels  584 us (48%)
  waiting for transfers between devices  329 us (27%)
  matrix products  150 us (12%)
  other arithmetic  93.3 us (8%)
  blocking collectives  29.1 us (2%)
  between operations  14.1 us (1%)
  local copies, waits for them, and re-layouts  13.8 us (1%)
    pallas_call x1, Pallas kernels, mlp_phase(): pl.pallas_call(functools.partial(mlp_kernel, n_chunks), out_shape=jax.Sha...  584 us
    psum x1, waiting for transfers between devices, local_layer(): attn_sum = lax.psum(attn_part, 'mx')  159 us
    all_gather x1, waiting for transfers between devices, local_layer(): attn_all = lax.all_gather(attn_loc, 'my', axis=0, tiled=True)  74.5 us
    reduce_scatter x1, waiting for transfers between devices, local_layer(): q_loc = lax.psum_scatter(q_part, 'my', scatter_dimension=0, tiled=True)  73.4 us
    dot_general x1, matrix products, attend_local(): jnp.einsum('qkgt,tkd->qkgd', attn_prob, v_full, preferred_element_type=jn...  46.9 us
    dot_general x1, matrix products, attend_local(): jnp.einsum('qkgd,tkd->qkgt', q_grp, k_full, preferred_element_type=jnp.fl...  43.2 us
    reduce_sum x1, other arithmetic, attend_local(): attn_prob = jax.nn.softmax(scores, axis=-1).astype(jnp.bfloat16)  37.5 us
    psum x2, blocking collectives, width_norm(): lax.psum(jnp.sum(values_f * values_f, axis=-1, keepdims=True), 'my')  29.1 us
  transfers between devices with their start and end apart: 7, of which 5 were waited for; matrix products, arithmetic and copies ran while one was open for 10% of the time, Pallas kernels for 0%

profile of v1, /device:TPU:97, one launch (start us, length us, event | category | flops | bytes accessed | tf_op | source)
XLA Modules:
  0.0 1213.4 jit_solution(812815157921717472)
XLA Ops:
  6.6 8.1 fusion.7
  14.7 15.9 %psum.21 = f32[4096,1]{0,1:T(1,128)S(1)} all-reduce(f32[4096,1]{0,1:T(1,128)S(1)} %bitcast.66), channel_id=1, replica_groups=mesh['dp'=1,'my'=4,'mx'=8] {'my'}, use_global_device_ids=true, to_apply=%region_1.0 | all-reduce | flops 4096 | bytes 32768 | tf_op jit(solution)/shard_map/psum | solution.py:364
  30.7 8.9 fusion.18
  39.7 8.4 fusion.17
  48.4 20.7 %fusion.14 = bf16[4096,7,128]{2,0,1:T(8,128)(2,1)} fusion(bf16[1792,7,128]{2,0,1:T(8,128)(2,1)S(1)} %copy-done.2, bf16[4096,1792]{1,0:T(8,128)(2,1)} %param.10, f32[1792]{0:T(1024)S(1)} %convert_element_type.82, f32[4096]{0:T(1024)S(1)} %bitcast.69), kind=kOutput, calls=%fused_computation.24 | convolution fusion | flops 13186367488 | bytes 25254912 | tf_op jit(solution)/shard_map/td,dhe->the/dot_general | solution.py:373
  70.3 1.2 fusion.34
  72.3 1.9 multiply_cosine_fusion
  74.2 5.7 iota_compare_fusion
  79.9 5.6 reduce-scatter.4.cloned.1.call-done
  85.9 73.4 %reduce-scatter.8.cloned.1.call-done = bf16[1024,7,128]{2,0,1:T(8,128)(2,1)} async-done(((bf16[4096,7,128]{2,0,1:T(8,128)(2,1)}), bf16[1024,7,128]{2,0,1:T(8,128)(2,1)}) %reduce-scatter.8.cloned.1.call-update) | async-done | bytes 1835024 | tf_op jit(solution)/shard_map/reduce_scatter | solution.py:376
  159.3 1.7 convert_element_type.91
  161.0 2.5 subtract_convert_fusion
  163.5 16.3 %all-gather.7.cloned.1.call-done = bf16[4096,1,128]{0,2,1:T(8,128)(2,1)} async-done(((bf16[1024,1,128]{0,2,1:T(8,128)(2,1)}), bf16[4096,1,128]{0,2,1:T(8,128)(2,1)}) %all-gather.7.cloned.1.call-update) | async-done | bytes 1048592 | tf_op jit(solution)/shard_map/all_gather | solution.py:382
  179.9 43.2 %fusion.1 = (f32[1024,7]{0,1:T(8,128)S(1)}, f32[4096,1024,7]{1,0,2:T(8,128)}) fusion(pred[1024,4096]{0,1:T(8,128)(4,1)} %iota_compare_fusion, bf16[1024,7,64]{2,0,1:T(8,128)(2,1)} %get-tuple-element.8, bf16[1024,7,64]{2,0,1:T(8,128)(2,1)S(1)} %get-tuple-element.7, bf16[4096,1,128]{0,2,1:T(8,128)(2,1)} %all-gather.7.cloned.1.call-done), kind=kOutput, calls=%fused_computation.4 | convolution fusion | flops 7607936000 | bytes 124547072 | tf_op jit(solution)/shard_map/qkgd,tkd->qkgt/dot_general | solution.py:34
  223.1 37.5 %fusion = f32[1024,7]{0,1:T(8,128)S(1)} fusion(f32[4096,1024,7]{1,0,2:T(8,128)} %get-tuple-element.14, f32[1024,7]{0,1:T(8,128)S(1)} %get-tuple-element.13, pred[1024,4096]{0,1:T(8,128)(4,1)} %iota_compare_fusion), kind=kLoop, calls=%fused_computation.3 | loop fusion | flops 117433344 | bytes 121692160 | tf_op jit(solution)/shard_map/reduce_sum | solution.py:38
  260.6 46.9 %convert_bitcast_fusion = bf16[1024,1,7,128]{0,3,2,1:T(8,128)(2,1)} fusion(f32[1024,7]{0,1:T(8,128)S(1)} %fusion, f32[1024,7]{0,1:T(8,128)S(1)} %get-tuple-element.13, f32[4096,1024,7]{1,0,2:T(8,128)} %get-tuple-element.14, pred[1024,4096]{0,1:T(8,128)(4,1)} %iota_compare_fusion, bf16[4096,1,128]{2,0,1:T(8,128)(2,1)} %all-gather.5.cloned.1.call-done), kind=kOutput, calls=%fused_computation.35 | convolution fusion | flops 7663910912 | bytes 124575744 | tf_op jit(solution)/shard_map/qkgt,tkd->qkgd/dot_general | solution.py:39
  307.7 74.5 %all-gather.9.cloned.1.call-done = bf16[4096,1,7,128]{0,3,2,1:T(8,128)(2,1)} async-done(((bf16[1024,1,7,128]{0,3,2,1:T(8,128)(2,1)}), bf16[4096,1,7,128]{0,3,2,1:T(8,128)(2,1)}) %all-gather.9.cloned.1.call-update) | async-done | bytes 7340048 | tf_op jit(solution)/shard_map/all_gather | solution.py:385
  382.2 21.8 %bitcast_convert_fusion = bf16[4096,1792]{1,0:T(8,128)(2,1)} fusion(bf16[7,128,1792]{2,1,0:T(8,128)(2,1)S(1)} %copy-done.3, bf16[4096,1,7,128]{0,3,2,1:T(8,128)(2,1)} %all-gather.9.cloned.1.call-done), kind=kOutput, calls=%fused_computation.19 | convolution fusion | flops 13160677376 | bytes 25231360 | tf_op jit(solution)/shard_map/the,hed->td/dot_general | solution.py:386
  404.7 158.7 %all-reduce.2.cloned.1.call-done = bf16[4096,1792]{1,0:T(8,128)(2,1)} async-done(((bf16[4096,1792]{1,0:T(8,128)(2,1)}), bf16[4096,1792]{1,0:T(8,128)(2,1)}) %all-reduce.2.cloned.1.call-update) | async-done | bytes 14680080 | tf_op jit(solution)/shard_map/psum | solution.py:387
  563.4 18.2 %fusion.4 = (f32[4096]{0:T(1024)S(1)}, bf16[4096,1792]{1,0:T(8,128)(2,1)}) fusion(bf16[4096,1792]{1,0:T(8,128)(2,1)} %all-reduce.2.cloned.1.call-done, bf16[4096,1792]{1,0:T(8,128)(2,1)} %param.10), kind=kLoop, calls=%fused_computation.12 | loop fusion | flops 51376128 | bytes 44056576 | tf_op jit(solution)/shard_map/reduce_sum | solution.py:364
  581.5 13.2 %psum.23 = f32[4096,1]{0,1:T(1,128)S(1)} all-reduce(f32[4096,1]{0,1:T(1,128)S(1)} %bitcast.64), channel_id=1, replica_groups=mesh['dp'=1,'my'=4,'mx'=8] {'my'}, use_global_device_ids=true, to_apply=%region_9.10 | all-reduce | flops 4096 | bytes 32768 | tf_op jit(solution)/shard_map/psum | solution.py:364
  594.7 14.7 %fusion.6.m_hbm = bf16[4096,1792]{1,0:T(8,128)(2,1)} fusion(bf16[4096,1792]{1,0:T(8,128)(2,1)} %get-tuple-element.6.h_hbm, f32[1792]{0:T(1024)S(1)} %convert_element_type.100, f32[4096]{0:T(1024)S(1)} %bitcast.65), kind=kLoop, calls=%fused_computation.14 | loop fusion | flops 29360128 | bytes 29383680 | tf_op jit(solution)/shard_map/convert_element_type | solution.py:365
  609.4 583.6 %mlp_phase.1 = bf16[4096,1792]{1,0:T(8,128)(2,1)} custom-call(bf16[4096,1792]{1,0:T(8,128)(2,1)} %fusion.6.m_hbm, bf16[4096,1792]{1,0:T(8,128)(2,1)} %get-tuple-element.6.h_hbm, bf16[1792,2560]{1,0:T(8,128)(2,1)} %wg_hbm.1, bf16[1792,2560]{1,0:T(8,128)(2,1)} %wu_hbm.1, bf16[2560,1792]{1,0:T(8,128)(2,1)} %wd_hbm.1), custom_call_target="tpu_custom_call" | custom-call | tf_op jit(solution)/shard_map/mlp_phase/pallas_call | solution.py:341
  1193.0 13.1 %copy.31 = bf16[4096,1792]{1,0:T(8,128)(2,1)} copy(bf16[4096,1792]{1,0:T(8,128)(2,1)} %mlp_phase.1) | data formatting | bytes 29360128
  (35 shorter events, 3.7 us)
Async XLA Ops:
  6.5 24.1 %copy-start = (bf16[1792]{0:T(1024)(128)(2,1)S(1)}, bf16[1792]{0:T(1024)(128)(2,1)}, u32[]{:S(2)}) copy-start(bf16[1792]{0:T(1024)(128)(2,1)} %param.11) | copy-start | bytes 10756
  6.5 24.1 %copy-start.4 = (bf16[1792,1,128]{2,0,1:T(8,128)(2,1)S(1)}, bf16[1792,1,128]{2,0,1:T(8,128)(2,1)}, u32[]{:S(2)}) copy-start(bf16[1792,1,128]{2,0,1:T(8,128)(2,1)} %param.13) | copy-start | bytes 1376260
  6.6 62.7 %reduce-scatter.6.cloned.1.call-start = ((), (), s32[]{:S(2)}) async-start(), calls=%async_computation.5 | async-start | bytes 1310720 | tf_op jit(solution)/shard_map/reduce_scatter | solution.py:377
  39.6 8.8 copy-start.2
  39.6 45.9 %reduce-scatter.4.cloned.1.call-start = ((), (), s32[]{:S(2)}) async-start(), calls=%async_computation.3 | async-start | bytes 1310720 | tf_op jit(solution)/shard_map/reduce_scatter | solution.py:378
  48.2 111.1 %reduce-scatter.8.cloned.1.call-start = ((), (), s32[]{:S(2)}) async-start(), calls=%async_computation.7 | async-start | bytes 9175040 | tf_op jit(solution)/shard_map/reduce_scatter | solution.py:376
  69.2 110.7 %all-gather.7.cloned.1.call-start = ((), (), s32[]{:S(2)}) async-start(), calls=%async_computation.6 | async-start | bytes 1310720 | tf_op jit(solution)/shard_map/all_gather | solution.py:382
  72.3 188.4 %all-gather.5.cloned.1.call-start = ((), (), s32[]{:S(2)}) async-start(), calls=%async_computation.4 | async-start | bytes 1310720 | tf_op jit(solution)/shard_map/all_gather | solution.py:383
  85.6 296.6 %all-gather.9.cloned.1.call-start = ((), (), s32[]{:S(2)}) async-start(), calls=%async_computation.9 | async-start | bytes 9175040 | tf_op jit(solution)/shard_map/all_gather | solution.py:385
  260.6 121.6 %copy-start.3 = (bf16[7,128,1792]{2,1,0:T(8,128)(2,1)S(1)}, bf16[7,128,1792]{2,1,0:T(8,128)(2,1)}, u32[]{:S(2)}) copy-start(bf16[7,128,1792]{2,1,0:T(8,128)(2,1)} %param.15) | copy-start | bytes 9633796
  307.6 255.7 %all-reduce.2.cloned.1.call-start = ((), (), s32[]{:S(2)}) async-start(), calls=%async_computation.8 | async-start | bytes 29360128 | tf_op jit(solution)/shard_map/psum | solution.py:387
  404.0 0.7 copy-start.1
Sparse Core Ops, SparseCore 0:
  39.7 22.5 reduce-scatter.5
  64.6 20.8 reduce-scatter.3
  87.8 71.4 reduce-scatter.7
  160.7 19.0 all-gather.6
  181.3 21.8 all-gather.4
  307.8 74.3 all-gather.8
  404.2 159.1 all-reduce.1

commit v2 on v1

--- a/solution.py
+++ b/solution.py
@@ -13,31 +13,6 @@
 MESH = pl.DeviceIdType.MESH
 F32 = jnp.float32
 BF16 = jnp.bfloat16
-
-
-def apply_rope(values, positions):
-    half_dim = values.shape[-1] // 2
-    inv_freq = ROPE_BASE ** (-jnp.arange(half_dim, dtype=jnp.float32) / half_dim)
-    angles = positions[:, None] * inv_freq[None, :]
-    cos_t = jnp.cos(angles)[:, None, :]
-    sin_t = jnp.sin(angles)[:, None, :]
-    values_f = values.astype(jnp.float32)
-    first_half = values_f[..., :half_dim]
-    second_half = values_f[..., half_dim:]
-    return jnp.concatenate([first_half * cos_t - second_half * sin_t, second_half * cos_t + first_half * sin_t], axis=-1).astype(jnp.bfloat16)
-
-
-def attend_local(q_rot, k_full, v_full, query_pos):
-    q_tokens, heads_loc, head_dim = q_rot.shape
-    kv_loc = k_full.shape[1]
-    q_grp = q_rot.reshape(q_tokens, kv_loc, heads_loc // kv_loc, head_dim)
-    scores = jnp.einsum("qkgd,tkd->qkgt", q_grp, k_full, preferred_element_type=jnp.float32) * head_dim ** -0.5
-    key_pos = jnp.arange(k_full.shape[0])
-    causal = key_pos[None, :] <= query_pos[:, None]
-    scores = jnp.where(causal[:, None, None, :], scores, -jnp.inf)
-    attn_prob = jax.nn.softmax(scores, axis=-1).astype(jnp.bfloat16)
-    attn_out = jnp.einsum("qkgt,tkd->qkgd", attn_prob, v_full, preferred_element_type=jnp.float32)
-    return attn_out.astype(jnp.bfloat16).reshape(q_tokens, heads_loc, head_dim)
 
 
 class Place:
@@ -59,11 +34,11 @@
         self.dev_core = {"mx": self.x * 2 + (1 - self.core)}
         self.partners = (self.dev_yp, self.dev_ym, self.dev_xp, self.dev_xm, self.dev_core)
 
-    def entry(self):
+    def entry(self, extra=()):
         barrier = pltpu.get_barrier_semaphore()
-        for dev in self.partners:
+        for dev in self.partners + extra:
             pl.semaphore_signal(barrier, inc=1, device_id=dev, device_id_type=MESH)
-        pl.semaphore_wait(barrier, len(self.partners))
+        pl.semaphore_wait(barrier, len(self.partners) + len(extra))
 
     def give_credit(self, credit):
         for slot, dev in ((1, self.dev_yp), (0, self.dev_ym), (3, self.dev_xp), (2, self.dev_xm), (4, self.dev_core)):
@@ -167,7 +142,7 @@
         rcopy(other, other, dys.at[i], dyr.at[i], at.dev_core).wait_recv()
 
     def h_copy(c):
-        return pltpu.make_async_copy(h_hbm.at[rows(c * tc + own_half + at.x * xb, xb, xb)], H, h_sem)
+        return pltpu.make_async_copy(h_hbm.at[rows(c * xb, xb, xb)], H, h_sem)
 
     def y_copy(c):
         return pltpu.make_async_copy(YB, y_hbm.at[rows(c * tc, tc, tc)], y_sem)
@@ -329,7 +304,7 @@
             at.give_credit(credit)
 
 
-def mlp_phase(m_full, h_full, w_gate, w_up, w_down, chunk):
+def mlp_phase(m_full, h_own, w_gate, w_up, w_down, chunk):
     tokens, width = m_full.shape
     ff = w_gate.shape[1]
     n_chunks = tokens // chunk
@@ -353,41 +328,416 @@
         ],
         compiler_params=pltpu.CompilerParams(collective_id=1, has_side_effects=True, vmem_limit_bytes=67043328),
         name="mlp_phase",
-    )(m_full, h_full, w_gate, w_up, w_down)
+    )(m_full, h_own, w_gate, w_up, w_down)
+
+
+def attn_kernel(n_chunks, x_hbm, ga, gm, cos_t, sin_t, wq_hbm, wk_hbm, wv_hbm, wo_hbm, m_hbm, h_hbm,
+                WQKV, WO, X, N, QP, R1, R2, QS, KV, O, WP, DR, XR1, XR2, XH, HB, MO, SQ, RC, ST1, ST2,
+                w_sem, x_sem, xh_sem, hb_sem, mo_sem, credit,
+                t1s, t1r, s1s, s1r, s2s, s2r, kvs, kvr, ocs, ocr, ofs, ofr, dds, ddr, x1s, x1r, x2s, x2r, t2s, t2r, xas, xar, xfs, xfr, dms, dmr):
+    at = Place()
+    tc, width = N.shape
+    full_width = width * 4
+    qkv_w = WQKV.shape[1]
+    head = 128
+    heads = QS.shape[1] // (tc // 4)
+    q_w = heads * head
+    qb = tc // 4
+    hq = qb // 2
+    hb = tc // 2
+    xb = hb // 4
+    hx = xb // 2
+    own_half = at.core * hb
+    my_rows = own_half + at.x * xb
+    peers = ((at.dev_yp, at.yp), (at.dev_ym, at.ym), ({"my": at.yo}, at.yo))
+    blk = min(128, tc)
+    n_blk = tc // blk
+    step = 16
+
+    w_copies = [
+        pltpu.make_async_copy(wq_hbm, WQKV.at[:, pl.ds(0, q_w)], w_sem.at[0]),
+        pltpu.make_async_copy(wk_hbm, WQKV.at[:, pl.ds(q_w, head)], w_sem.at[1]),
+        pltpu.make_async_copy(wv_hbm, WQKV.at[:, pl.ds(q_w + head, head)], w_sem.at[2]),
+        pltpu.make_async_copy(wo_hbm, WO, w_sem.at[3]),
+    ]
+
+    def x_copy(c):
+        return pltpu.make_async_copy(x_hbm.at[rows(c * tc, tc, tc)], X.at[c % 2], x_sem.at[c % 2])
+
+    x_copy(0).start()
+    for c in w_copies:
+        c.start()
+    at.entry(extra=({"my": at.yo},))
+
+    def slot(c):
+        return c % 4
+
+    def pair(c):
+        return c % 2
+
+    def stats_copies(st, ssem, rsem, c):
+        own = st.at[c, at.y]
+        return [rcopy(own, own, ssem.at[pair(c), i], rsem.at[c, i], dev) for i, (dev, _) in enumerate(peers)]
+
+    def s1_copies(c):
+        s, o = slot(c), at.yo * qb
+        return [rcopy(QP.at[s, rows(o, hq, hq)], R1.at[s, 0], s1s.at[pair(c), 0], s1r.at[s, 0], at.dev_yp),
+                rcopy(QP.at[s, rows(o + hq, hq, hq)], R1.at[s, 1], s1s.at[pair(c), 1], s1r.at[s, 1], at.dev_ym)]
+
+    def s2_copies(c):
+        s = slot(c)
+        return [rcopy(QP.at[s, rows(at.yp * qb, qb, qb)], R2.at[s, 0], s2s.at[pair(c), 0], s2r.at[s, 0], at.dev_yp),
+                rcopy(QP.at[s, rows(at.ym * qb, qb, qb)], R2.at[s, 1], s2s.at[pair(c), 1], s2r.at[s, 1], at.dev_ym)]
+
+    def kv_copies(c):
+        own = KV.at[rows(c * tc + at.y * qb, qb, qb)]
+        return [rcopy(own, own, kvs.at[pair(c), i], kvr.at[c, i], dev) for i, (dev, _) in enumerate(peers)]
+
+    def o_copies(c):
+        s = slot(c)
+        own = O.at[s, rows(at.y * qb, qb, qb)]
+        return [rcopy(own, own, ocs.at[pair(c), 0], ocr.at[s, 0], at.dev_yp), rcopy(own, own, ocs.at[pair(c), 1], ocr.at[s, 1], at.dev_ym)]
+
+    def of_copies(c):
+        s = slot(c)
+        a = O.at[s, rows(at.ym * qb, hq, hq)]
+        b = O.at[s, rows(at.yp * qb + hq, hq, hq)]
+        return [rcopy(a, a, ofs.at[pair(c), 0], ofr.at[s, 0], at.dev_yp), rcopy(b, b, ofs.at[pair(c), 1], ofr.at[s, 1], at.dev_ym)]
+
+    def dd_copies(c):
+        s = slot(c)
+        return [rcopy(WP.at[s, rows((1 - at.core) * hb, hb, hb)], DR.at[s], dds.at[pair(c)], ddr.at[s], at.dev_core)]
+
+    def x1_copies(c):
+        s, o = slot(c), own_half + at.xo * xb
+        return [rcopy(WP.at[s, rows(o, hx, hx)], XR1.at[s, 0], x1s.at[pair(c), 0], x1r.at[s, 0], at.dev_xp),
+                rcopy(WP.at[s, rows(o + hx, hx, hx)], XR1.at[s, 1], x1s.at[pair(c), 1], x1r.at[s, 1], at.dev_xm)]
+
+    def x2_copies(c):
+        s = slot(c)
+        return [rcopy(WP.at[s, rows(own_half + at.xp * xb, xb, xb)], XR2.at[s, 0], x2s.at[pair(c), 0], x2r.at[s, 0], at.dev_xp),
+                rcopy(WP.at[s, rows(own_half + at.xm * xb, xb, xb)], XR2.at[s, 1], x2s.at[pair(c), 1], x2r.at[s, 1], at.dev_xm)]
+
+    def m_rows(c, start, size):
+        return m_hbm.at[rows(c * tc + start, size, size)]
+
+    def xa_copies(c):
+        src, dst = MO.at[slot(c)], m_rows(c, my_rows, xb)
+        return [rcopy(src, dst, xas.at[pair(c), 0], xar.at[c, 0], at.dev_xp), rcopy(src, dst, xas.at[pair(c), 1], xar.at[c, 1], at.dev_xm)]
+
+    def xf_copies(c):
+        a = m_rows(c, own_half + at.xm * xb, hx)
+        b = m_rows(c, own_half + at.xp * xb + hx, hx)
+        return [rcopy(a, a, xfs.at[pair(c), 0], xfr.at[c, 0], at.dev_xp), rcopy(b, b, xfs.at[pair(c), 1], xfr.at[c, 1], at.dev_xm)]
+
+    def dm_copy(c, i):
+        if i == 0:
+            return rcopy(MO.at[slot(c)], m_rows(c, my_rows, xb), dms.at[pair(c), 0], dmr.at[c, 0], at.dev_core)
+        b = m_rows(c, own_half + (at.xm, at.xp, at.xo)[i - 1] * xb, xb)
+        return rcopy(b, b, dms.at[pair(c), i], dmr.at[c, i], at.dev_core)
+
+    def dm_wait_recv(c, i):
+        b = m_rows(c, (1 - at.core) * hb + (at.x, at.xm, at.xp, at.xo)[i] * xb, xb)
+        rcopy(b, b, dms.at[pair(c), i], dmr.at[c, i], at.dev_core).wait_recv()
+
+    def xh_copy(c):
+        return pltpu.make_async_copy(x_hbm.at[rows(c * tc + my_rows, xb, xb)], XH.at[pair(c)], xh_sem.at[pair(c)])
+
+    def hb_copy(c):
+        return pltpu.make_async_copy(HB.at[slot(c)], h_hbm.at[rows(c * xb, xb, xb)], hb_sem.at[pair(c)])
+
+    def mo_copy(c):
+        return pltpu.make_async_copy(MO.at[slot(c)], m_rows(c, my_rows, xb), mo_sem.at[pair(c)])
+
+    def start(copies):
+        for cp in copies:
+            cp.start()
+
+    def wait(copies):
+        for cp in copies:
+            cp.wait()
+
+    def as_row(col_b):
+        r, l = col_b.shape
+        eye = lax.broadcasted_iota(jnp.int32, (r, l), 0) == lax.broadcasted_iota(jnp.int32, (r, l), 1)
+        return jnp.sum(jnp.where(eye, col_b, 0.0), axis=0, keepdims=True)
+
+    def as_col(row, r):
+        l = row.shape[1]
+        eye = lax.broadcasted_iota(jnp.int32, (r, l), 0) == lax.broadcasted_iota(jnp.int32, (r, l), 1)
+        return jnp.sum(jnp.where(eye, jnp.broadcast_to(row, (r, l)), 0.0), axis=1, keepdims=True)
+
+    def square_sum(v):
+        vf = v.astype(F32)
+        return jnp.sum(vf * vf, axis=-1, keepdims=True)
+
+    def inv_rms(st, c):
+        tot = (st[c, 0] + st[c, 1]) + (st[c, 2] + st[c, 3])
+        return lax.rsqrt(tot / full_width + NORM_EPS)
+
+    def stage(k, s, body):
+        c = k - s
+
+        @pl.when(jnp.logical_and(c >= 0, c < n_chunks))
+        def _():
+            body(c)
+
+    def st_sumsq(c):
+        x_copy(c).wait()
+
+        @pl.loop(0, tc // step)
+        def _(i):
+            r = rows(i * step, step, step)
+            SQ[r, :] = jnp.broadcast_to(square_sum(X[c % 2, r, :]), (step, 128))
+
+        parts = [as_row(SQ[b * blk:(b + 1) * blk, :]) for b in range(n_blk)]
+        parts = parts + [jnp.zeros_like(parts[0])] * (8 - n_blk)
+        ST1[c, at.y] = jnp.concatenate(parts, axis=0)
+        start(stats_copies(ST1, t1s, t1r, c))
+
+    def st_qkv(c):
+        wait(stats_copies(ST1, t1s, t1r, c))
+        inv = inv_rms(ST1, c)
+        for b in range(n_blk):
+            RC[b * blk:(b + 1) * blk, :] = jnp.broadcast_to(as_col(inv[b:b + 1, :], blk), (blk, 128))
+
+        @pl.loop(0, tc // step)
+        def _(i):
+            r = rows(i * step, step, step)
+            N[r, :] = (X[c % 2, r, :].astype(F32) * RC[r, 0:1] * ga[...]).astype(BF16)
+
+        n_t = qkv_w // 384
+
+        @pl.loop(0, n_t)
+        def _(n):
+            cols = rows(n * 384, 384, 128)
+            QP[slot(c), :, cols] = jnp.dot(N[...], WQKV[:, cols], preferred_element_type=F32).astype(BF16)
+
+        start(s1_copies(c))
+
+    def st_add1(c):
+        wait(s1_copies(c))
+        s = slot(c)
+
+        @pl.loop(0, hq // step)
+        def _(i):
+            ri = rows(i * step, step, step)
+            ra = rows(at.yp * qb + i * step, step, step)
+            rb = rows(at.ym * qb + hq + i * step, step, step)
+            QP[s, ra, :] = (QP[s, ra, :].astype(F32) + R1[s, 0, ri, :].astype(F32)).astype(BF16)
+            QP[s, rb, :] = (QP[s, rb, :].astype(F32) + R1[s, 1, ri, :].astype(F32)).astype(BF16)
+
+        start(s2_copies(c))
+
+    def st_rope(c):
+        wait(s2_copies(c))
+        s = slot(c)
+        own = rows(at.y * qb, qb, qb)
+        cos_v = cos_t[rows(c * qb, qb, qb), :]
+        sin_v = sin_t[rows(c * qb, qb, qb), :]
+
+        def piece(i):
+            cols = slice(i * head, (i + 1) * head)
+            v = QP[s, own, cols].astype(F32) + R2[s, 0, :, cols].astype(F32) + R2[s, 1, :, cols].astype(F32)
+            return v.astype(BF16)
+
+        def turned(i):
+            v = piece(i).astype(F32)
+            return (v * cos_v + pltpu.roll(v, head // 2, 1) * sin_v).astype(BF16)
+
+        kv_rows = rows(c * tc + at.y * qb, qb, qb)
+        KV[kv_rows, 0:head] = turned(heads)
+        KV[kv_rows, head:2 * head] = piece(heads + 1)
+        start(kv_copies(c))
+        for i in range(heads):
+            QS[pair(c), i * qb:(i + 1) * qb, :] = turned(i)
+
+    def st_attend(c):
+        wait(kv_copies(c))
+        q = QS[pair(c)]
+        scale = head ** -0.5 * 1.4426950408889634
+
+        def scores(j):
+            keys = KV[rows(j * tc, tc, tc), 0:head]
+            return lax.dot_general(q, keys, (((1,), (1,)), ((), ())), preferred_element_type=F32) * scale
+
+        def values(j, p):
+            return jnp.dot(p.astype(BF16), KV[rows(j * tc, tc, tc), head:2 * head], preferred_element_type=F32)
+
+        qpos = at.y * qb + lax.broadcasted_iota(jnp.int32, (qb, tc), 0)
+        keep = lax.broadcasted_iota(jnp.int32, (qb, tc), 1) <= qpos
+        sc = scores(c).reshape(heads, qb, tc)
+        sc = jnp.where(keep[None], sc, -jnp.inf).reshape(heads * qb, tc)
+        top = jnp.max(sc, axis=-1, keepdims=True)
+        p = jnp.exp2(sc - top)
+
+        def more(j, carry):
+            top, total, acc = carry
+            sc = scores(j)
+            new = jnp.maximum(top, jnp.max(sc, axis=-1, keepdims=True))
+            fade = jnp.exp2(top - new)
+            p = jnp.exp2(sc - new)
+            return new, total * fade + jnp.sum(p, axis=-1, keepdims=True), acc * fade + values(j, p)
+
+        top, total, acc = lax.fori_loop(0, c, more, (top, jnp.sum(p, axis=-1, keepdims=True), values(c, p)))
+        out = (acc / total).astype(BF16)
+        for i in range(heads):
+            O[slot(c), rows(at.y * qb, qb, qb), i * head:(i + 1) * head] = out[i * qb:(i + 1) * qb, :]
+        start(o_copies(c))
+
+    def st_ofwd(c):
+        wait(o_copies(c))
+        start(of_copies(c))
+
+    def st_oproj(c):
+        wait(of_copies(c))
+        dn_w = 256 if width % 256 == 0 else 128
+
+        @pl.loop(0, width // dn_w)
+        def _(n):
+            cols = rows(n * dn_w, dn_w, 128)
+            WP[slot(c), :, cols] = jnp.dot(O[slot(c)], WO[:, cols], preferred_element_type=F32).astype(BF16)
+
+        start(dd_copies(c))
+
+    def st_x1(c):
+        wait(dd_copies(c))
+        s = slot(c)
+
+        @pl.loop(0, hb // step)
+        def _(i):
+            ri = rows(i * step, step, step)
+            ra = rows(own_half + i * step, step, step)
+            WP[s, ra, :] = (WP[s, ra, :].astype(F32) + DR[s, ri, :].astype(F32)).astype(BF16)
+
+        start(x1_copies(c))
+
+    def st_x2(c):
+        xh_copy(c).start()
+        wait(x1_copies(c))
+        s = slot(c)
+        ra = rows(own_half + at.xp * xb, hx, hx)
+        rb = rows(own_half + at.xm * xb + hx, hx, hx)
+        WP[s, ra, :] = (WP[s, ra, :].astype(F32) + XR1[s, 0].astype(F32)).astype(BF16)
+        WP[s, rb, :] = (WP[s, rb, :].astype(F32) + XR1[s, 1].astype(F32)).astype(BF16)
+        start(x2_copies(c))
+
+    def st_h(c):
+        wait(x2_copies(c))
+        xh_copy(c).wait()
+        s = slot(c)
+        total = WP[s, rows(my_rows, xb, xb), :].astype(F32) + XR2[s, 0].astype(F32) + XR2[s, 1].astype(F32)
+        h = (XH[pair(c)].astype(F32) + total).astype(BF16)
+        HB[s] = h
+        row = as_row(jnp.broadcast_to(square_sum(h), (xb, 128)))
+        ST2[c, at.y] = jnp.broadcast_to(row, (8, 128))
+        start(stats_copies(ST2, t2s, t2r, c))
+        hb_copy(c).start()
+
+    def st_m(c):
+        wait(stats_copies(ST2, t2s, t2r, c))
+        hb_copy(c).wait()
+        s = slot(c)
+        inv = as_col(inv_rms(ST2, c)[0:1, :], xb)
+        MO[s] = (HB[s].astype(F32) * inv * gm[...]).astype(BF16)
+        start(xa_copies(c))
+        dm_copy(c, 0).start()
+        mo_copy(c).start()
+
+    def st_xf(c):
+        wait(xa_copies(c))
+        dm_copy(c, 0).wait_send()
+        mo_copy(c).wait()
+        start(xf_copies(c))
+        dm_copy(c, 1).start()
+        dm_copy(c, 2).start()
+
+    def st_dm(c):
+        wait(xf_copies(c))
+        dm_copy(c, 1).wait_send()
+        dm_copy(c, 2).wait_send()
+        dm_copy(c, 3).start()
+
+    def st_end(c):
+        dm_copy(c, 3).wait_send()
+        for i in range(4):
+            dm_wait_recv(c, i)
+
+    bodies = (st_sumsq, st_qkv, st_add1, st_rope, st_attend, st_ofwd, st_oproj, st_x1, st_x2, st_h, st_m, st_xf, st_dm, st_end)
+    n_iter = n_chunks + len(bodies) - 1
+    for cp in w_copies:
+        cp.wait()
+
+    @pl.loop(0, n_iter)
+    def _(k):
+        @pl.when(k >= 2)
+        def _():
+            at.take_credit(credit)
+
+        for s, body in enumerate(bodies):
+            stage(k, s, body)
+            if s == 1:
+                @pl.when(k + 1 < n_chunks)
+                def _():
+                    x_copy(k + 1).start()
+
+        @pl.when(k < n_iter - 2)
+        def _():
+            at.give_credit(credit)
+
+
+def attn_phase(x_in, gain_attn, gain_mlp, cos_t, sin_t, w_q, w_k, w_v, w_o, chunk):
+    tokens, width = x_in.shape
+    q_w = w_q.shape[1]
+    heads = q_w // 128
+    n_chunks = tokens // chunk
+    qb, hb = chunk // 4, chunk // 2
+    xb = hb // 4
+    hbm = pl.BlockSpec(memory_space=pl.ANY)
+    vmem = pl.BlockSpec(memory_space=pltpu.VMEM)
+    sem = pltpu.SemaphoreType.DMA
+    vm = lambda *s: pltpu.VMEM(s, BF16)
+    vf = lambda *s: pltpu.VMEM(s, F32)
+    qkv_w = q_w + 256
+    return pl.pallas_call(
+        functools.partial(attn_kernel, n_chunks),
+        out_shape=(jax.ShapeDtypeStruct((tokens, width), BF16), jax.ShapeDtypeStruct((tokens // 8, width), BF16)),
+        in_specs=[hbm, vmem, vmem, vmem, vmem, hbm, hbm, hbm, hbm],
+        out_specs=(hbm, hbm),
+        scratch_shapes=[
+            vm(width, qkv_w), vm(q_w, width), vm(2, chunk, width), vm(chunk, width), vm(4, chunk, qkv_w),
+            vm(4, 2, qb // 2, qkv_w), vm(4, 2, qb, qkv_w), vm(2, heads * qb, 128), vm(tokens, 256), vm(4, chunk, q_w),
+            vm(4, chunk, width), vm(4, hb, width), vm(4, 2, xb // 2, width), vm(4, 2, xb, width), vm(2, xb, width), vm(4, xb, width), vm(4, xb, width),
+            vf(chunk, 128), vf(chunk, 128), vf(n_chunks, 4, 8, 128), vf(n_chunks, 4, 8, 128),
+            sem((4,)), sem((2,)), sem((2,)), sem((2,)), sem((2,)), pltpu.SemaphoreType.REGULAR((5,)),
+            sem((2, 3)), sem((n_chunks, 3)), sem((2, 2)), sem((4, 2)), sem((2, 2)), sem((4, 2)), sem((2, 3)), sem((n_chunks, 3)),
+            sem((2, 2)), sem((4, 2)), sem((2, 2)), sem((4, 2)), sem((2,)), sem((4,)), sem((2, 2)), sem((4, 2)), sem((2, 2)), sem((4, 2)),
+            sem((2, 3)), sem((n_chunks, 3)), sem((2, 2)), sem((n_chunks, 2)), sem((2, 2)), sem((n_chunks, 2)), sem((2, 4)), sem((n_chunks, 4)),
+        ],
+        compiler_params=pltpu.CompilerParams(collective_id=2, has_side_effects=True, vmem_limit_bytes=67043328),
+        name="attn_phase",
+    )(x_in, gain_attn, gain_mlp, cos_t, sin_t, w_q, w_k, w_v, w_o)
 
 
 def solution(mesh, chunk=CHUNK):
     my_size = mesh.shape["my"]
 
-    def width_norm(values, gain, width):
-        values_f = values.astype(jnp.float32)
-        row_sq = lax.psum(jnp.sum(values_f * values_f, axis=-1, keepdims=True), "my")
-        return (values_f * lax.rsqrt(row_sq / width + NORM_EPS) * gain.astype(jnp.float32)).astype(jnp.bfloat16)
-
     def local_layer(x_in, gain_attn, w_q, w_k, w_v, w_o, gain_mlp, w_gate, w_up, w_down):
-        tokens = x_in.shape[0]
-        width = x_in.shape[1] * my_size
-        q_tokens = tokens // my_size
-        row_idx = lax.axis_index("my")
-        normed = width_norm(x_in, gain_attn, width)
-        q_part = jnp.einsum("td,dhe->the", normed, w_q, preferred_element_type=jnp.float32).astype(jnp.bfloat16)
-        k_part = jnp.einsum("td,dhe->the", normed, w_k, preferred_element_type=jnp.float32).astype(jnp.bfloat16)
-        v_part = jnp.einsum("td,dhe->the", normed, w_v, preferred_element_type=jnp.float32).astype(jnp.bfloat16)
-        q_loc = lax.psum_scatter(q_part, "my", scatter_dimension=0, tiled=True)
-        k_loc = lax.psum_scatter(k_part, "my", scatter_dimension=0, tiled=True)
-        v_loc = lax.psum_scatter(v_part, "my", scatter_dimension=0, tiled=True)
-        query_pos = row_idx * q_tokens + jnp.arange(q_tokens)
-        q_rot = apply_rope(q_loc, query_pos.astype(jnp.float32))
-        k_rot = apply_rope(k_loc, query_pos.astype(jnp.float32))
-        k_full = lax.all_gather(k_rot, "my", axis=0, tiled=True)
-        v_full = lax.all_gather(v_loc, "my", axis=0, tiled=True)
-        attn_loc = attend_local(q_rot, k_full, v_full, query_pos)
-        attn_all = lax.all_gather(attn_loc, "my", axis=0, tiled=True)
-        attn_part = jnp.einsum("the,hed->td", attn_all, w_o, preferred_element_type=jnp.float32).astype(jnp.bfloat16)
-        attn_sum = lax.psum(attn_part, "mx")
-        residual = (x_in.astype(jnp.float32) + attn_sum.astype(jnp.float32)).astype(jnp.bfloat16)
-        normed_mlp = width_norm(residual, gain_mlp, width)
-        return mlp_phase(normed_mlp, residual, w_gate, w_up, w_down, chunk)
+        tokens, width = x_in.shape
+        head = w_q.shape[-1]
+        qb = chunk // my_size
+        row = jnp.arange(tokens // my_size)
+        positions = (row // qb) * chunk + lax.axis_index("my") * qb + row % qb
+        half = head // 2
+        inv_freq = ROPE_BASE ** (-jnp.arange(half, dtype=F32) / half)
+        angles = positions.astype(F32)[:, None] * inv_freq[None, :]
+        cos_h, sin_h = jnp.cos(angles), jnp.sin(angles)
+        cos_t = jnp.concatenate([cos_h, cos_h], axis=-1)
+        sin_t = jnp.concatenate([-sin_h, sin_h], axis=-1)
+        m_full, h_own = attn_phase(
+            x_in, gain_attn.astype(F32).reshape(1, width), gain_mlp.astype(F32).reshape(1, width), cos_t, sin_t,
+            w_q.reshape(width, -1), w_k.reshape(width, -1), w_v.reshape(width, -1), w_o.reshape(-1, width), chunk)
+        return mlp_phase(m_full, h_own, w_gate, w_up, w_down, chunk)
 
     in_specs = (P("dp", "my"), P("my"), P("my", "mx", None), P("my", "mx", None), P("my", "mx", None), P("mx", None, "my"), P("my"), P("my", "mx"), P("my", "mx"), P("mx", "my"))
     return jax.shard_map(local_layer, mesh=mesh, in_specs=in_specs, out_specs=P("dp", "my"), check_vma=False)

time: 1220 us -> 895 us (0.73)
  waiting for transfers between devices: 329 us -> 0 us
  Pallas kernels: 584 us -> 868 us
  matrix products: 150 us -> 0 us
  other arithmetic: 93.3 us -> 3.26 us
  blocking collectives: 29.1 us -> 0 us
  between operations: 14.1 us -> 0.04 us
    pallas_call x0 -> x1, Pallas kernels: none -> 285 us  [attn_phase(): pl.pallas_call(functools.partial(attn_kernel, n_chunks), out_shape=(jax.S...]
    psum x1 -> x0, waiting for transfers between devices: 159 us -> none  [local_layer(): attn_sum = lax.psum(attn_part, 'mx')]
    dot_general x6 -> x0, matrix products: 150 us -> none  [the longest x1 46.9 us: attend_local(): jnp.einsum('qkgt,tkd->qkgd', attn_prob, v_full, preferred_element_type=jn...]
    all_gather x3 -> x0, waiting for transfers between devices: 90.8 us -> none  [the longest x1 74.5 us: local_layer(): attn_all = lax.all_gather(attn_loc, 'my', axis=0, tiled=True)]
    reduce_scatter x3 -> x0, waiting for transfers between devices: 79 us -> none  [the longest x1 73.4 us: local_layer(): q_loc = lax.psum_scatter(q_part, 'my', scatter_dimension=0, tiled=True)]
    reduce_sum x3 -> x0, other arithmetic: 63.8 us -> none  [the longest x1 37.5 us: attend_local(): attn_prob = jax.nn.softmax(scores, axis=-1).astype(jnp.bfloat16)]
    psum x2 -> x0, blocking collectives: 29.1 us -> none  [width_norm(): lax.psum(jnp.sum(values_f * values_f, axis=-1, keepdims=True), 'my')]
    convert_element_type x6 -> x1, other arithmetic: 17.4 us -> 0.01 us  [local_layer(): angles = positions.astype(F32)[:, None] * inv_freq[None, :]]
  transfers between devices with their start and end apart: 7 -> 0, of which waited for: 5 -> 0; matrix products, arithmetic and copies ran while one was open for 10% -> 0% of each run, Pallas kernels for 0% -> 0%
where the time goes in v2:
time: 895 us
  Pallas kernels  868 us (97%)
  local copies, waits for them, and re-layouts  23.6 us (3%)
    pallas_call x1, Pallas kernels, mlp_phase(): pl.pallas_call(functools.partial(mlp_kernel, n_chunks), out_shape=jax.Sha...  583 us
    pallas_call x1, Pallas kernels, attn_phase(): pl.pallas_call(functools.partial(attn_kernel, n_chunks), out_shape=(jax.S...  285 us

profile of v2, /device:TPU:97, one launch (start us, length us, event | category | flops | bytes accessed | tf_op | source)
XLA Modules:
  0.0 894.8 jit_solution(13681299721724568567)
XLA Ops:
  0.0 1.3 reshape.61.ga
  1.3 1.3 reshape.63.gm
  2.6 1.9 fusion
  4.5 1.3 pad_maximum_fusion
  5.9 4.3 copy.12
  10.2 3.6 copy.13.wq_hbm
  13.8 285.0 %attn_phase.1 = (bf16[4096,1792]{1,0:T(8,128)(2,1)}, bf16[512,1792]{1,0:T(8,128)(2,1)}) custom-call(bf16[4096,1792]{1,0:T(8,128)(2,1)} %x_hbm.1, f32[1,1792]{1,0:T(1,128)} %reshape.61.ga, f32[1,1792]{1,0:T(1,128)} %reshape.63.gm, f32[1024,128]{1,0:T(8,128)} %get-tuple-element.12.cos_t, f32[1024,128]{1,0:T(8,128)} %get-tuple-element.13.sin_t, ...), custom_call_target="tpu_custom_call" | custom-call | tf_op jit(solution)/shard_map/attn_phase/pallas_call | solution.py:702
  298.8 582.8 %mlp_phase.1 = bf16[4096,1792]{1,0:T(8,128)(2,1)} custom-call(bf16[4096,1792]{1,0:T(8,128)(2,1)} %get-tuple-element.7.m_hbm, bf16[512,1792]{1,0:T(8,128)(2,1)} %get-tuple-element.8.h_hbm, bf16[1792,2560]{1,0:T(8,128)(2,1)} %wg_hbm.1, bf16[1792,2560]{1,0:T(8,128)(2,1)} %wu_hbm.1, bf16[2560,1792]{1,0:T(8,128)(2,1)} %wd_hbm.1), custom_call_target="tpu_custom_call" | custom-call | tf_op jit(solution)/shard_map/mlp_phase/pallas_call | solution.py:316
  881.7 13.1 %copy.15 = bf16[4096,1792]{1,0:T(8,128)(2,1)} copy(bf16[4096,1792]{1,0:T(8,128)(2,1)} %mlp_phase.1) | data formatting | bytes 29360128
  (2 shorter events, 0.0 us)

commit v3 on v2

--- a/solution.py
+++ b/solution.py
@@ -10,6 +10,7 @@
 ROPE_BASE = 10000.0
 NORM_EPS = 1e-6
 CHUNK = 512
+EARLY = 2
 MESH = pl.DeviceIdType.MESH
 F32 = jnp.float32
 BF16 = jnp.bfloat16
@@ -32,6 +33,9 @@
         self.dev_xp = {"mx": self.xp * 2 + self.core}
         self.dev_xm = {"mx": self.xm * 2 + self.core}
         self.dev_core = {"mx": self.x * 2 + (1 - self.core)}
+        self.dev_yo = {"my": self.yo}
+        self.ys = (self.dev_yp, self.dev_ym)
+        self.xs = (self.dev_xp, self.dev_xm)
         self.partners = (self.dev_yp, self.dev_ym, self.dev_xp, self.dev_xm, self.dev_core)
 
     def entry(self, extra=()):
@@ -53,12 +57,52 @@
     return pltpu.make_async_remote_copy(src_ref=src, dst_ref=dst, send_sem=send_sem, recv_sem=recv_sem, device_id=dev, device_id_type=MESH)
 
 
+def as_row(col_b):
+    eye = lax.broadcasted_iota(jnp.int32, col_b.shape, 0) == lax.broadcasted_iota(jnp.int32, col_b.shape, 1)
+    return jnp.sum(jnp.where(eye, col_b, 0.0), axis=0, keepdims=True)
+
+
+def as_col(row, r):
+    shape = (r, row.shape[1])
+    eye = lax.broadcasted_iota(jnp.int32, shape, 0) == lax.broadcasted_iota(jnp.int32, shape, 1)
+    return jnp.sum(jnp.where(eye, jnp.broadcast_to(row, shape), 0.0), axis=1, keepdims=True)
+
+
+def square_sum(v):
+    vf = v.astype(F32)
+    return jnp.sum(vf * vf, axis=-1, keepdims=True)
+
+
+def inv_rms(st, c, full_width):
+    tot = (st[c, 0] + st[c, 1]) + (st[c, 2] + st[c, 3])
+    return lax.rsqrt(tot / full_width + NORM_EPS)
+
+
+def two(srcs, dsts, send, recv, devs):
+    return [rcopy(src, dst, send.at[i], recv.at[i], dev) for i, (src, dst, dev) in enumerate(zip(srcs, dsts, devs))]
+
+
+def slots(ref):
+    return [ref.at[i] for i in range(2)]
+
+
+def start(copies):
+    for c in copies:
+        c.start()
+
+
+def wait(copies):
+    for c in copies:
+        c.wait()
+
+
 def rows(start, size, align):
     return pl.ds(pl.multiple_of(start, align), size)
 
 
-def mlp_kernel(n_chunks, m_hbm, h_hbm, wg_hbm, wu_hbm, wd_hbm, y_hbm, WG, WU, WD, M, PP, R1, R2, ACT, DP, DR, XR1, XR2, YB, H,
-               w_sem, m_sem, h_sem, y_sem, credit, s1s, s1r, s2s, s2r, acs, acr, fws, fwr, dds, ddr, x1s, x1r, x2s, x2r, xas, xar, xfs, xfr, dys, dyr):
+def mlp_kernel(n_chunks, x_hbm, gains, me_hbm, he_hbm, wp_hbm, wg_hbm, wu_hbm, wd_hbm, y_hbm, ml_hbm, hl_hbm,
+               WG, WU, WD, M, PP, R1, R2, ACT, DP, DR, XR1, XR2, YB, H, OP, OR, OX1, OX2, XH, HB, MO, ST,
+               w_sem, m_sem, h_sem, y_sem, o_sem, ods, odr, oxs, oxr, ots, otr, oms, omr, credit, s1s, s1r, s2s, s2r, acs, acr, fws, fwr, dds, ddr, x1s, x1r, x2s, x2r, xas, xar, xfs, xfr, dys, dyr):
     at = Place()
     tc, width = M.shape
     ff = WG.shape[1]
@@ -71,15 +115,29 @@
     gu_w = ff // gu_tiles
     dn_w = 256 if width % 256 == 0 else 128
 
-    w_copies = [pltpu.make_async_copy(s, d, w_sem.at[i]) for i, (s, d) in enumerate(((wg_hbm, WG), (wu_hbm, WU), (wd_hbm, WD)))]
-    for c in w_copies:
-        c.start()
-
-    def m_copy(c):
-        return pltpu.make_async_copy(m_hbm.at[rows(c * tc, tc, tc)], M, m_sem)
-
-    m_copy(0).start()
-    at.entry()
+    def m_wait():
+        pltpu.make_async_copy(me_hbm.at[pl.ds(0, tc)], M, m_sem).wait()
+
+    def m_start(c):
+        @pl.when(c < EARLY)
+        def _():
+            pltpu.make_async_copy(me_hbm.at[rows(c * tc, tc, tc)], M, m_sem).start()
+
+        @pl.when(c >= EARLY)
+        def _():
+            pltpu.make_async_copy(ml_hbm.at[rows((c - EARLY) * tc, tc, tc)], M, m_sem).start()
+
+    def gu_copies(n):
+        cols = rows(n * gu_w, gu_w, 128)
+        return [pltpu.make_async_copy(wg_hbm.at[:, cols], WG.at[:, cols], w_sem.at[n]),
+                pltpu.make_async_copy(wu_hbm.at[:, cols], WU.at[:, cols], w_sem.at[gu_tiles + n])]
+
+    wd_copy = pltpu.make_async_copy(wd_hbm, WD, w_sem.at[2 * gu_tiles])
+    pltpu.make_async_copy(me_hbm.at[pl.ds(0, tc)], M, m_sem).start()
+    for n in range(gu_tiles):
+        start(gu_copies(n))
+    wd_copy.start()
+    at.entry(extra=(at.dev_yo,))
 
     def gu_part(par, lo, hi):
         @pl.loop(lo, hi)
@@ -90,21 +148,18 @@
 
     def s1_copies(par):
         o = at.yo * qb
-        return (rcopy(PP.at[par, rows(o, hq, hq)], R1.at[0], s1s.at[0], s1r.at[0], at.dev_yp),
-                rcopy(PP.at[par, rows(o + hq, hq, hq)], R1.at[1], s1s.at[1], s1r.at[1], at.dev_ym))
+        return two([PP.at[par, rows(r, hq, hq)] for r in (o, o + hq)], slots(R1), s1s, s1r, at.ys)
 
     def s2_copies(par):
-        return (rcopy(PP.at[par, rows(at.yp * qb, qb, qb)], R2.at[par, 0], s2s.at[par, 0], s2r.at[par, 0], at.dev_yp),
-                rcopy(PP.at[par, rows(at.ym * qb, qb, qb)], R2.at[par, 1], s2s.at[par, 1], s2r.at[par, 1], at.dev_ym))
+        return two([PP.at[par, rows(b * qb, qb, qb)] for b in (at.yp, at.ym)], slots(R2.at[par]), s2s.at[par], s2r.at[par], at.ys)
 
     def act_copies(par):
-        own = ACT.at[par, rows(at.y * qb, qb, qb)]
-        return (rcopy(own, own, acs.at[0], acr.at[0], at.dev_yp), rcopy(own, own, acs.at[1], acr.at[1], at.dev_ym))
+        own = [ACT.at[par, rows(at.y * qb, qb, qb)]] * 2
+        return two(own, own, acs, acr, at.ys)
 
     def fwd_copies(par):
-        a = ACT.at[par, rows(at.ym * qb, hq, hq)]
-        b = ACT.at[par, rows(at.yp * qb + hq, hq, hq)]
-        return (rcopy(a, a, fws.at[par, 0], fwr.at[par, 0], at.dev_yp), rcopy(b, b, fws.at[par, 1], fwr.at[par, 1], at.dev_ym))
+        half = [ACT.at[par, rows(r, hq, hq)] for r in (at.ym * qb, at.yp * qb + hq)]
+        return two(half, half, fws.at[par], fwr.at[par], at.ys)
 
     def dd_copy():
         return rcopy(DP.at[rows((1 - at.core) * hb, hb, hb)], DR, dds, ddr, at.dev_core)
@@ -113,24 +168,21 @@
 
     def x1_copies():
         o = own_half + at.xo * xb
-        return (rcopy(DP.at[rows(o, hx, hx)], XR1.at[0], x1s.at[0], x1r.at[0], at.dev_xp),
-                rcopy(DP.at[rows(o + hx, hx, hx)], XR1.at[1], x1s.at[1], x1r.at[1], at.dev_xm))
+        return two([DP.at[rows(r, hx, hx)] for r in (o, o + hx)], slots(XR1), x1s, x1r, at.xs)
 
     def x2_copies():
-        return (rcopy(DP.at[rows(own_half + at.xp * xb, xb, xb)], XR2.at[0], x2s.at[0], x2r.at[0], at.dev_xp),
-                rcopy(DP.at[rows(own_half + at.xm * xb, xb, xb)], XR2.at[1], x2s.at[1], x2r.at[1], at.dev_xm))
+        return two([DP.at[rows(own_half + b * xb, xb, xb)] for b in (at.xp, at.xm)], slots(XR2), x2s, x2r, at.xs)
 
     def yblk(b):
         return YB.at[rows(own_half + b * xb, xb, xb)]
 
     def xa_copies():
-        own = yblk(at.x)
-        return (rcopy(own, own, xas.at[0], xar.at[0], at.dev_xp), rcopy(own, own, xas.at[1], xar.at[1], at.dev_xm))
+        own = [yblk(at.x)] * 2
+        return two(own, own, xas, xar, at.xs)
 
     def xf_copies():
-        a = YB.at[rows(own_half + at.xm * xb, hx, hx)]
-        b = YB.at[rows(own_half + at.xp * xb + hx, hx, hx)]
-        return (rcopy(a, a, xfs.at[0], xfr.at[0], at.dev_xp), rcopy(b, b, xfs.at[1], xfr.at[1], at.dev_xm))
+        half = [YB.at[rows(own_half + r, hx, hx)] for r in (at.xm * xb, at.xp * xb + hx)]
+        return two(half, half, xfs, xfr, at.xs)
 
     def dy_copy(i):
         b = (at.x, at.xm, at.xp, at.xo)[i]
@@ -141,25 +193,141 @@
         other = YB.at[rows((1 - at.core) * hb + b * xb, xb, xb)]
         rcopy(other, other, dys.at[i], dyr.at[i], at.dev_core).wait_recv()
 
-    def h_copy(c):
-        return pltpu.make_async_copy(h_hbm.at[rows(c * xb, xb, xb)], H, h_sem)
+    def h_wait():
+        pltpu.make_async_copy(he_hbm.at[pl.ds(0, xb)], H, h_sem).wait()
+
+    def h_start(c):
+        @pl.when(c < EARLY)
+        def _():
+            pltpu.make_async_copy(he_hbm.at[rows(c * xb, xb, xb)], H, h_sem).start()
+
+        @pl.when(c >= EARLY)
+        def _():
+            pltpu.make_async_copy(hl_hbm.at[rows((c - EARLY) * xb, xb, xb)], H, h_sem).start()
 
     def y_copy(c):
         return pltpu.make_async_copy(YB, y_hbm.at[rows(c * tc, tc, tc)], y_sem)
 
-    def start(copies):
-        for c in copies:
-            c.start()
-
-    def wait(copies):
-        for c in copies:
-            c.wait()
-
-    w_copies[0].wait()
-    w_copies[1].wait()
-    m_copy(0).wait()
-    gu_part(0, 0, gu_tiles)
-    w_copies[2].wait()
+    my_rows = own_half + at.x * xb
+    peers = at.ys + (at.dev_yo,)
+
+    def od_copy(c):
+        return rcopy(wp_hbm.at[rows((c - EARLY) * tc + (1 - at.core) * hb, hb, hb)], OR, ods, odr, at.dev_core)
+
+    def op_copy(c):
+        return pltpu.make_async_copy(wp_hbm.at[rows((c - EARLY) * tc + own_half, hb, hb)], OP, o_sem.at[0])
+
+    def xh_copy(c):
+        return pltpu.make_async_copy(x_hbm.at[rows(c * tc + my_rows, xb, xb)], XH, o_sem.at[1])
+
+    def hl_copy(c):
+        return pltpu.make_async_copy(HB, hl_hbm.at[rows((c - EARLY) * xb, xb, xb)], o_sem.at[2])
+
+    def ml_rows(c, first, size):
+        return ml_hbm.at[rows((c - EARLY) * tc + first, size, size)]
+
+    def mo_copy(c):
+        return pltpu.make_async_copy(MO, ml_rows(c, my_rows, xb), o_sem.at[3])
+
+    def o1_copies():
+        return two([OP.at[rows(at.xo * xb + r, hx, hx)] for r in (0, hx)], slots(OX1), oxs.at[0], oxr.at[0], at.xs)
+
+    def o2_copies():
+        return two([OP.at[rows(b * xb, xb, xb)] for b in (at.xp, at.xm)], slots(OX2), oxs.at[1], oxr.at[1], at.xs)
+
+    def ot_copies(c):
+        own = ST.at[c, at.y]
+        return [rcopy(own, own, ots.at[i], otr.at[c, i], dev) for i, dev in enumerate(peers)]
+
+    def oa_copies(c):
+        return two([MO] * 2, [ml_rows(c, my_rows, xb)] * 2, oxs.at[2], oxr.at[2], at.xs)
+
+    def of_copies(c):
+        half = [ml_rows(c, own_half + r, hx) for r in (at.xm * xb, at.xp * xb + hx)]
+        return two(half, half, oxs.at[3], oxr.at[3], at.xs)
+
+    def om_copy(c, i):
+        b = ml_rows(c, own_half + (at.x, at.xm, at.xp, at.xo)[i] * xb, xb)
+        return rcopy(MO if i == 0 else b, b, oms.at[i], omr.at[i], at.dev_core)
+
+    def om_wait_recv(c, i):
+        b = ml_rows(c, (1 - at.core) * hb + (at.x, at.xm, at.xp, at.xo)[i] * xb, xb)
+        rcopy(b, b, oms.at[i], omr.at[i], at.dev_core).wait_recv()
+
+    def o_begin(c):
+        od_copy(c).start()
+        op_copy(c).start()
+        xh_copy(c).start()
+
+    def o_core(c):
+        od_copy(c).wait()
+        op_copy(c).wait()
+
+        @pl.loop(0, hb // 16)
+        def _(i):
+            r = rows(i * 16, 16, 16)
+            OP[r, :] = (OP[r, :].astype(F32) + OR[r, :].astype(F32)).astype(BF16)
+
+        start(o1_copies())
+
+    def o_ring(c):
+        wait(o1_copies())
+        ra = rows(at.xp * xb, hx, hx)
+        rb = rows(at.xm * xb + hx, hx, hx)
+        OP[ra, :] = (OP[ra, :].astype(F32) + OX1[0].astype(F32)).astype(BF16)
+        OP[rb, :] = (OP[rb, :].astype(F32) + OX1[1].astype(F32)).astype(BF16)
+        start(o2_copies())
+
+    def o_sum(c):
+        wait(o2_copies())
+        xh_copy(c).wait()
+        total = OP[rows(at.x * xb, xb, xb), :].astype(F32) + OX2[0].astype(F32) + OX2[1].astype(F32)
+        h = (XH[...].astype(F32) + total).astype(BF16)
+        HB[...] = h
+        ST[c, at.y] = jnp.broadcast_to(as_row(jnp.broadcast_to(square_sum(h), (xb, 128))), (8, 128))
+        start(ot_copies(c))
+        hl_copy(c).start()
+
+    def o_norm(c):
+        wait(ot_copies(c))
+        hl_copy(c).wait()
+        inv = as_col(inv_rms(ST, c, width * 4)[0:1, :], xb)
+        MO[...] = (HB[...].astype(F32) * inv * gains[1:2, :]).astype(BF16)
+        start(oa_copies(c))
+        om_copy(c, 0).start()
+        mo_copy(c).start()
+
+    def o_pass(c):
+        wait(oa_copies(c))
+        mo_copy(c).wait()
+        start(of_copies(c))
+        om_copy(c, 1).start()
+        om_copy(c, 2).start()
+
+    def o_last(c):
+        wait(of_copies(c))
+        om_copy(c, 3).start()
+
+    def o_end(c):
+        for i in range(4):
+            om_copy(c, i).wait_send()
+            om_wait_recv(c, i)
+
+    m_wait()
+    for i, b in enumerate((at.yo, at.yp, at.ym, at.y)):
+        br = rows(b * qb, qb, qb)
+
+        @pl.loop(0, gu_tiles)
+        def _(n):
+            if i == 0:
+                wait(gu_copies(n))
+            g_cols = rows(n * gu_w, gu_w, 128)
+            PP[0, br, g_cols] = jnp.dot(M[br, :], WG[:, g_cols], preferred_element_type=F32).astype(BF16)
+            PP[0, br, rows(ff + n * gu_w, gu_w, 128)] = jnp.dot(M[br, :], WU[:, g_cols], preferred_element_type=F32).astype(BF16)
+
+        if i == 0:
+            start(s1_copies(0))
+    wd_copy.wait()
 
     @pl.loop(0, n_chunks + 2)
     def _(k):
@@ -174,17 +342,26 @@
         def _():
             at.take_credit(credit)
 
-        @pl.when(has_s)
+        @pl.when(jnp.logical_and(has_s, k >= 1))
         def _():
             start(s1_copies(par))
 
-        @pl.when(has_gu)
-        def _():
-            m_copy(k + 1).start()
-
         @pl.when(has_d)
         def _():
-            h_copy(k - 2).start()
+            h_start(k - 2)
+
+        def o_step(body):
+            @pl.when(k + EARLY < n_chunks)
+            def _():
+                body(k + EARLY)
+
+        def m_step(body):
+            @pl.when(jnp.logical_and(k + 1 >= EARLY, has_gu))
+            def _():
+                body(k + 1)
+
+        o_step(o_begin)
+        m_step(o_norm)
 
         @pl.when(has_a)
         def _():
@@ -202,6 +379,8 @@
 
             start(act_copies(alt))
 
+        m_step(o_pass)
+
         @pl.when(has_d)
         def _():
             wait(fwd_copies(par))
@@ -212,6 +391,9 @@
                 DP[:, cols] = jnp.dot(ACT[par], WD[:, cols], preferred_element_type=F32).astype(BF16)
 
             dd_copy().start()
+
+        o_step(o_core)
+        m_step(o_last)
 
         @pl.when(has_s)
         def _():
@@ -228,6 +410,13 @@
 
             start(s2_copies(par))
 
+        o_step(o_ring)
+        m_step(o_end)
+
+        @pl.when(has_gu)
+        def _():
+            m_start(k + 1)
+
         @pl.when(has_d)
         def _():
             dd_copy().wait()
@@ -243,8 +432,10 @@
 
         @pl.when(has_gu)
         def _():
-            m_copy(k + 1).wait()
+            m_wait()
             gu_part(alt, 0, 2)
+
+        o_step(o_sum)
 
         @pl.when(has_d)
         def _():
@@ -267,7 +458,7 @@
         @pl.when(has_d)
         def _():
             wait(x2_copies())
-            h_copy(k - 2).wait()
+            h_wait()
             r = rows(own_half + at.x * xb, xb, xb)
             down = DP[r, :].astype(F32) + XR2[0].astype(F32) + XR2[1].astype(F32)
             YB[r, :] = (H[...].astype(F32) + down).astype(BF16)
@@ -304,36 +495,39 @@
             at.give_credit(credit)
 
 
-def mlp_phase(m_full, h_own, w_gate, w_up, w_down, chunk):
-    tokens, width = m_full.shape
+def mlp_phase(x_in, gains, m_early, h_early, o_part, w_gate, w_up, w_down, chunk):
+    tokens, width = x_in.shape
     ff = w_gate.shape[1]
     n_chunks = tokens // chunk
     qb, hb = chunk // 4, chunk // 2
     xb = hb // 4
     hbm = pl.BlockSpec(memory_space=pl.ANY)
     sem = pltpu.SemaphoreType.DMA
+    S2, P2 = sem((2,)), sem((2, 2))
     vm = lambda *s: pltpu.VMEM(s, BF16)
     return pl.pallas_call(
         functools.partial(mlp_kernel, n_chunks),
-        out_shape=jax.ShapeDtypeStruct((tokens, width), BF16),
-        in_specs=[hbm] * 5,
-        out_specs=hbm,
+        out_shape=tuple(jax.ShapeDtypeStruct((n, width), BF16) for n in (tokens, tokens - EARLY * chunk, tokens // 8 - EARLY * xb)),
+        in_specs=[hbm, pl.BlockSpec(memory_space=pltpu.VMEM)] + [hbm] * 6,
+        out_specs=(hbm, hbm, hbm),
         scratch_shapes=[
             vm(width, ff), vm(width, ff), vm(ff, width), vm(chunk, width), vm(2, chunk, 2 * ff),
             vm(2, qb // 2, 2 * ff), vm(2, 2, qb, 2 * ff), vm(2, chunk, ff), vm(chunk, width), vm(hb, width),
             vm(2, xb // 2, width), vm(2, xb, width), vm(chunk, width), vm(xb, width),
-            sem((3,)), sem, sem, sem, pltpu.SemaphoreType.REGULAR((5,)),
-            sem((2,)), sem((2,)), sem((2, 2)), sem((2, 2)), sem((2,)), sem((2,)), sem((2, 2)), sem((2, 2)),
-            sem, sem, sem((2,)), sem((2,)), sem((2,)), sem((2,)), sem((2,)), sem((2,)), sem((2,)), sem((2,)), sem((4,)), sem((4,)),
+            vm(hb, width), vm(hb, width), vm(2, xb // 2, width), vm(2, xb, width), vm(xb, width), vm(xb, width), vm(xb, width),
+            pltpu.VMEM((n_chunks, 4, 8, 128), F32),
+            sem((11,)), sem, sem, sem, sem((4,)), sem, sem, sem((4, 2)), sem((4, 2)), sem((3,)), sem((n_chunks, 3)), sem((4,)), sem((4,)), pltpu.SemaphoreType.REGULAR((5,)),
+            S2, S2, P2, P2, S2, S2, P2, P2,
+            sem, sem, S2, S2, S2, S2, S2, S2, S2, S2, sem((4,)), sem((4,)),
         ],
         compiler_params=pltpu.CompilerParams(collective_id=1, has_side_effects=True, vmem_limit_bytes=67043328),
         name="mlp_phase",
-    )(m_full, h_own, w_gate, w_up, w_down)
-
-
-def attn_kernel(n_chunks, x_hbm, ga, gm, cos_t, sin_t, wq_hbm, wk_hbm, wv_hbm, wo_hbm, m_hbm, h_hbm,
+    )(x_in, gains, m_early, h_early, o_part, w_gate, w_up, w_down)[0]
+
+
+def attn_kernel(n_chunks, x_hbm, gains, cos_t, sin_t, wq_hbm, wk_hbm, wv_hbm, wo_hbm, m_hbm, h_hbm, wp_hbm,
                 WQKV, WO, X, N, QP, R1, R2, QS, KV, O, WP, DR, XR1, XR2, XH, HB, MO, SQ, RC, ST1, ST2,
-                w_sem, x_sem, xh_sem, hb_sem, mo_sem, credit,
+                w_sem, x_sem, xh_sem, hb_sem, mo_sem, wp_sem, credit,
                 t1s, t1r, s1s, s1r, s2s, s2r, kvs, kvr, ocs, ocr, ofs, ofr, dds, ddr, x1s, x1r, x2s, x2r, t2s, t2r, xas, xar, xfs, xfr, dms, dmr):
     at = Place()
     tc, width = N.shape
@@ -349,17 +543,15 @@
     hx = xb // 2
     own_half = at.core * hb
     my_rows = own_half + at.x * xb
-    peers = ((at.dev_yp, at.yp), (at.dev_ym, at.ym), ({"my": at.yo}, at.yo))
+    peers = at.ys + (at.dev_yo,)
     blk = min(128, tc)
     n_blk = tc // blk
     step = 16
 
     w_copies = [
-        pltpu.make_async_copy(wq_hbm, WQKV.at[:, pl.ds(0, q_w)], w_sem.at[0]),
-        pltpu.make_async_copy(wk_hbm, WQKV.at[:, pl.ds(q_w, head)], w_sem.at[1]),
-        pltpu.make_async_copy(wv_hbm, WQKV.at[:, pl.ds(q_w + head, head)], w_sem.at[2]),
-        pltpu.make_async_copy(wo_hbm, WO, w_sem.at[3]),
-    ]
+        pltpu.make_async_copy(w, WQKV.at[:, pl.ds(i * head, head)], w_sem.at[i])
+        for i, w in enumerate([wq_hbm.at[h] for h in range(heads)] + [wk_hbm, wv_hbm])
+    ] + [pltpu.make_async_copy(wo_hbm, WO, w_sem.at[heads + 2])]
 
     def x_copy(c):
         return pltpu.make_async_copy(x_hbm.at[rows(c * tc, tc, tc)], X.at[c % 2], x_sem.at[c % 2])
@@ -367,7 +559,7 @@
     x_copy(0).start()
     for c in w_copies:
         c.start()
-    at.entry(extra=({"my": at.yo},))
+    at.entry(extra=(at.dev_yo,))
 
     def slot(c):
         return c % 4
@@ -377,32 +569,27 @@
 
     def stats_copies(st, ssem, rsem, c):
         own = st.at[c, at.y]
-        return [rcopy(own, own, ssem.at[pair(c), i], rsem.at[c, i], dev) for i, (dev, _) in enumerate(peers)]
+        return [rcopy(own, own, ssem.at[pair(c), i], rsem.at[c, i], dev) for i, dev in enumerate(peers)]
 
     def s1_copies(c):
         s, o = slot(c), at.yo * qb
-        return [rcopy(QP.at[s, rows(o, hq, hq)], R1.at[s, 0], s1s.at[pair(c), 0], s1r.at[s, 0], at.dev_yp),
-                rcopy(QP.at[s, rows(o + hq, hq, hq)], R1.at[s, 1], s1s.at[pair(c), 1], s1r.at[s, 1], at.dev_ym)]
+        return two([QP.at[s, rows(r, hq, hq)] for r in (o, o + hq)], slots(R1.at[s]), s1s.at[pair(c)], s1r.at[s], at.ys)
 
     def s2_copies(c):
         s = slot(c)
-        return [rcopy(QP.at[s, rows(at.yp * qb, qb, qb)], R2.at[s, 0], s2s.at[pair(c), 0], s2r.at[s, 0], at.dev_yp),
-                rcopy(QP.at[s, rows(at.ym * qb, qb, qb)], R2.at[s, 1], s2s.at[pair(c), 1], s2r.at[s, 1], at.dev_ym)]
+        return two([QP.at[s, rows(b * qb, qb, qb)] for b in (at.yp, at.ym)], slots(R2.at[s]), s2s.at[pair(c)], s2r.at[s], at.ys)
 
     def kv_copies(c):
         own = KV.at[rows(c * tc + at.y * qb, qb, qb)]
-        return [rcopy(own, own, kvs.at[pair(c), i], kvr.at[c, i], dev) for i, (dev, _) in enumerate(peers)]
+        return [rcopy(own, own, kvs.at[pair(c), i], kvr.at[c, i], dev) for i, dev in enumerate(peers)]
 
     def o_copies(c):
-        s = slot(c)
-        own = O.at[s, rows(at.y * qb, qb, qb)]
-        return [rcopy(own, own, ocs.at[pair(c), 0], ocr.at[s, 0], at.dev_yp), rcopy(own, own, ocs.at[pair(c), 1], ocr.at[s, 1], at.dev_ym)]
+        own = [O.at[slot(c), rows(at.y * qb, qb, qb)]] * 2
+        return two(own, own, ocs.at[pair(c)], ocr.at[slot(c)], at.ys)
 
     def of_copies(c):
-        s = slot(c)
-        a = O.at[s, rows(at.ym * qb, hq, hq)]
-        b = O.at[s, rows(at.yp * qb + hq, hq, hq)]
-        return [rcopy(a, a, ofs.at[pair(c), 0], ofr.at[s, 0], at.dev_yp), rcopy(b, b, ofs.at[pair(c), 1], ofr.at[s, 1], at.dev_ym)]
+        half = [O.at[slot(c), rows(r, hq, hq)] for r in (at.ym * qb, at.yp * qb + hq)]
+        return two(half, half, ofs.at[pair(c)], ofr.at[slot(c)], at.ys)
 
     def dd_copies(c):
         s = slot(c)
@@ -410,25 +597,21 @@
 
     def x1_copies(c):
         s, o = slot(c), own_half + at.xo * xb
-        return [rcopy(WP.at[s, rows(o, hx, hx)], XR1.at[s, 0], x1s.at[pair(c), 0], x1r.at[s, 0], at.dev_xp),
-                rcopy(WP.at[s, rows(o + hx, hx, hx)], XR1.at[s, 1], x1s.at[pair(c), 1], x1r.at[s, 1], at.dev_xm)]
+        return two([WP.at[s, rows(r, hx, hx)] for r in (o, o + hx)], slots(XR1.at[s]), x1s.at[pair(c)], x1r.at[s], at.xs)
 
     def x2_copies(c):
         s = slot(c)
-        return [rcopy(WP.at[s, rows(own_half + at.xp * xb, xb, xb)], XR2.at[s, 0], x2s.at[pair(c), 0], x2r.at[s, 0], at.dev_xp),
-                rcopy(WP.at[s, rows(own_half + at.xm * xb, xb, xb)], XR2.at[s, 1], x2s.at[pair(c), 1], x2r.at[s, 1], at.dev_xm)]
+        return two([WP.at[s, rows(own_half + b * xb, xb, xb)] for b in (at.xp, at.xm)], slots(XR2.at[s]), x2s.at[pair(c)], x2r.at[s], at.xs)
 
     def m_rows(c, start, size):
         return m_hbm.at[rows(c * tc + start, size, size)]
 
     def xa_copies(c):
-        src, dst = MO.at[slot(c)], m_rows(c, my_rows, xb)
-        return [rcopy(src, dst, xas.at[pair(c), 0], xar.at[c, 0], at.dev_xp), rcopy(src, dst, xas.at[pair(c), 1], xar.at[c, 1], at.dev_xm)]
+        return two([MO.at[slot(c)]] * 2, [m_rows(c, my_rows, xb)] * 2, xas.at[pair(c)], xar.at[c], at.xs)
 
     def xf_copies(c):
-        a = m_rows(c, own_half + at.xm * xb, hx)
-        b = m_rows(c, own_half + at.xp * xb + hx, hx)
-        return [rcopy(a, a, xfs.at[pair(c), 0], xfr.at[c, 0], at.dev_xp), rcopy(b, b, xfs.at[pair(c), 1], xfr.at[c, 1], at.dev_xm)]
+        half = [m_rows(c, own_half + r, hx) for r in (at.xm * xb, at.xp * xb + hx)]
+        return two(half, half, xfs.at[pair(c)], xfr.at[c], at.xs)
 
     def dm_copy(c, i):
         if i == 0:
@@ -449,36 +632,13 @@
     def mo_copy(c):
         return pltpu.make_async_copy(MO.at[slot(c)], m_rows(c, my_rows, xb), mo_sem.at[pair(c)])
 
-    def start(copies):
-        for cp in copies:
-            cp.start()
-
-    def wait(copies):
-        for cp in copies:
-            cp.wait()
-
-    def as_row(col_b):
-        r, l = col_b.shape
-        eye = lax.broadcasted_iota(jnp.int32, (r, l), 0) == lax.broadcasted_iota(jnp.int32, (r, l), 1)
-        return jnp.sum(jnp.where(eye, col_b, 0.0), axis=0, keepdims=True)
-
-    def as_col(row, r):
-        l = row.shape[1]
-        eye = lax.broadcasted_iota(jnp.int32, (r, l), 0) == lax.broadcasted_iota(jnp.int32, (r, l), 1)
-        return jnp.sum(jnp.where(eye, jnp.broadcast_to(row, (r, l)), 0.0), axis=1, keepdims=True)
-
-    def square_sum(v):
-        vf = v.astype(F32)
-        return jnp.sum(vf * vf, axis=-1, keepdims=True)
-
-    def inv_rms(st, c):
-        tot = (st[c, 0] + st[c, 1]) + (st[c, 2] + st[c, 3])
-        return lax.rsqrt(tot / full_width + NORM_EPS)
+    def wp_copy(c):
+        return pltpu.make_async_copy(WP.at[slot(c)], wp_hbm.at[rows((c - EARLY) * tc, tc, tc)], wp_sem.at[pair(c)])
 
     def stage(k, s, body):
         c = k - s
 
-        @pl.when(jnp.logical_and(c >= 0, c < n_chunks))
+        @pl.when(jnp.logical_and(c >= 0, c < (EARLY if s >= 8 else n_chunks)))
         def _():
             body(c)
 
@@ -497,14 +657,19 @@
 
     def st_qkv(c):
         wait(stats_copies(ST1, t1s, t1r, c))
-        inv = inv_rms(ST1, c)
+
+        @pl.when(c == 0)
+        def _():
+            wait(w_copies[:-1])
+
+        inv = inv_rms(ST1, c, full_width)
         for b in range(n_blk):
             RC[b * blk:(b + 1) * blk, :] = jnp.broadcast_to(as_col(inv[b:b + 1, :], blk), (blk, 128))
 
         @pl.loop(0, tc // step)
         def _(i):
             r = rows(i * step, step, step)
-            N[r, :] = (X[c % 2, r, :].astype(F32) * RC[r, 0:1] * ga[...]).astype(BF16)
+            N[r, :] = (X[c % 2, r, :].astype(F32) * RC[r, 0:1] * gains[0:1, :]).astype(BF16)
 
         n_t = qkv_w // 384
 
@@ -591,6 +756,11 @@
 
     def st_oproj(c):
         wait(of_copies(c))
+
+        @pl.when(c == 0)
+        def _():
+            w_copies[-1].wait()
+
         dn_w = 256 if width % 256 == 0 else 128
 
         @pl.loop(0, width // dn_w)
@@ -598,9 +768,24 @@
             cols = rows(n * dn_w, dn_w, 128)
             WP[slot(c), :, cols] = jnp.dot(O[slot(c)], WO[:, cols], preferred_element_type=F32).astype(BF16)
 
-        start(dd_copies(c))
+        @pl.when(c < EARLY)
+        def _():
+            start(dd_copies(c))
+
+        @pl.when(c >= EARLY)
+        def _():
+            wp_copy(c).start()
 
     def st_x1(c):
+        @pl.when(c < EARLY)
+        def _():
+            st_x1_early(c)
+
+        @pl.when(c >= EARLY)
+        def _():
+            wp_copy(c).wait()
+
+    def st_x1_early(c):
         wait(dd_copies(c))
         s = slot(c)
 
@@ -638,8 +823,8 @@
         wait(stats_copies(ST2, t2s, t2r, c))
         hb_copy(c).wait()
         s = slot(c)
-        inv = as_col(inv_rms(ST2, c)[0:1, :], xb)
-        MO[s] = (HB[s].astype(F32) * inv * gm[...]).astype(BF16)
+        inv = as_col(inv_rms(ST2, c, full_width)[0:1, :], xb)
+        MO[s] = (HB[s].astype(F32) * inv * gains[1:2, :]).astype(BF16)
         start(xa_copies(c))
         dm_copy(c, 0).start()
         mo_copy(c).start()
@@ -664,9 +849,7 @@
             dm_wait_recv(c, i)
 
     bodies = (st_sumsq, st_qkv, st_add1, st_rope, st_attend, st_ofwd, st_oproj, st_x1, st_x2, st_h, st_m, st_xf, st_dm, st_end)
-    n_iter = n_chunks + len(bodies) - 1
-    for cp in w_copies:
-        cp.wait()
+    n_iter = max(n_chunks + 7, EARLY + len(bodies) - 1)
 
     @pl.loop(0, n_iter)
     def _(k):
@@ -686,37 +869,38 @@
             at.give_credit(credit)
 
 
-def attn_phase(x_in, gain_attn, gain_mlp, cos_t, sin_t, w_q, w_k, w_v, w_o, chunk):
+def attn_phase(x_in, gains, cos_t, sin_t, w_q, w_k, w_v, w_o, chunk):
     tokens, width = x_in.shape
-    q_w = w_q.shape[1]
-    heads = q_w // 128
+    heads = w_q.shape[0]
+    q_w = heads * 128
     n_chunks = tokens // chunk
     qb, hb = chunk // 4, chunk // 2
     xb = hb // 4
     hbm = pl.BlockSpec(memory_space=pl.ANY)
     vmem = pl.BlockSpec(memory_space=pltpu.VMEM)
     sem = pltpu.SemaphoreType.DMA
+    S2, P2 = sem((2,)), sem((2, 2))
     vm = lambda *s: pltpu.VMEM(s, BF16)
     vf = lambda *s: pltpu.VMEM(s, F32)
     qkv_w = q_w + 256
     return pl.pallas_call(
         functools.partial(attn_kernel, n_chunks),
-        out_shape=(jax.ShapeDtypeStruct((tokens, width), BF16), jax.ShapeDtypeStruct((tokens // 8, width), BF16)),
-        in_specs=[hbm, vmem, vmem, vmem, vmem, hbm, hbm, hbm, hbm],
-        out_specs=(hbm, hbm),
+        out_shape=tuple(jax.ShapeDtypeStruct((n, width), BF16) for n in (EARLY * chunk, EARLY * xb, tokens - EARLY * chunk)),
+        in_specs=[hbm, vmem, vmem, vmem, hbm, hbm, hbm, hbm],
+        out_specs=(hbm, hbm, hbm),
         scratch_shapes=[
             vm(width, qkv_w), vm(q_w, width), vm(2, chunk, width), vm(chunk, width), vm(4, chunk, qkv_w),
             vm(4, 2, qb // 2, qkv_w), vm(4, 2, qb, qkv_w), vm(2, heads * qb, 128), vm(tokens, 256), vm(4, chunk, q_w),
             vm(4, chunk, width), vm(4, hb, width), vm(4, 2, xb // 2, width), vm(4, 2, xb, width), vm(2, xb, width), vm(4, xb, width), vm(4, xb, width),
             vf(chunk, 128), vf(chunk, 128), vf(n_chunks, 4, 8, 128), vf(n_chunks, 4, 8, 128),
-            sem((4,)), sem((2,)), sem((2,)), sem((2,)), sem((2,)), pltpu.SemaphoreType.REGULAR((5,)),
-            sem((2, 3)), sem((n_chunks, 3)), sem((2, 2)), sem((4, 2)), sem((2, 2)), sem((4, 2)), sem((2, 3)), sem((n_chunks, 3)),
-            sem((2, 2)), sem((4, 2)), sem((2, 2)), sem((4, 2)), sem((2,)), sem((4,)), sem((2, 2)), sem((4, 2)), sem((2, 2)), sem((4, 2)),
-            sem((2, 3)), sem((n_chunks, 3)), sem((2, 2)), sem((n_chunks, 2)), sem((2, 2)), sem((n_chunks, 2)), sem((2, 4)), sem((n_chunks, 4)),
+            sem((heads + 3,)), S2, S2, S2, S2, S2, pltpu.SemaphoreType.REGULAR((5,)),
+            sem((2, 3)), sem((n_chunks, 3)), P2, sem((4, 2)), P2, sem((4, 2)), sem((2, 3)), sem((n_chunks, 3)),
+            P2, sem((4, 2)), P2, sem((4, 2)), S2, sem((4,)), P2, sem((4, 2)), P2, sem((4, 2)),
+            sem((2, 3)), sem((n_chunks, 3)), P2, sem((n_chunks, 2)), P2, sem((n_chunks, 2)), sem((2, 4)), sem((n_chunks, 4)),
         ],
         compiler_params=pltpu.CompilerParams(collective_id=2, has_side_effects=True, vmem_limit_bytes=67043328),
         name="attn_phase",
-    )(x_in, gain_attn, gain_mlp, cos_t, sin_t, w_q, w_k, w_v, w_o)
+    )(x_in, gains, cos_t, sin_t, w_q, w_k, w_v, w_o)
 
 
 def solution(mesh, chunk=CHUNK):
@@ -734,10 +918,10 @@
         cos_h, sin_h = jnp.cos(angles), jnp.sin(angles)
         cos_t = jnp.concatenate([cos_h, cos_h], axis=-1)
         sin_t = jnp.concatenate([-sin_h, sin_h], axis=-1)
-        m_full, h_own = attn_phase(
-            x_in, gain_attn.astype(F32).reshape(1, width), gain_mlp.astype(F32).reshape(1, width), cos_t, sin_t,
-            w_q.reshape(width, -1), w_k.reshape(width, -1), w_v.reshape(width, -1), w_o.reshape(-1, width), chunk)
-        return mlp_phase(m_full, h_own, w_gate, w_up, w_down, chunk)
+        gains = jnp.stack([gain_attn, gain_mlp]).astype(F32)
+        m_early, h_early, o_part = attn_phase(
+            x_in, gains, cos_t, sin_t, w_q.transpose(1, 0, 2), w_k.reshape(width, -1), w_v.reshape(width, -1), w_o.reshape(-1, width), chunk)
+        return mlp_phase(x_in, gains, m_early, h_early, o_part, w_gate, w_up, w_down, chunk)
 
     in_specs = (P("dp", "my"), P("my"), P("my", "mx", None), P("my", "mx", None), P("my", "mx", None), P("mx", None, "my"), P("my"), P("my", "mx"), P("my", "mx"), P("mx", "my"))
     return jax.shard_map(local_layer, mesh=mesh, in_specs=in_specs, out_specs=P("dp", "my"), check_vma=False)

time: 895 us -> 801 us (0.89)
  Pallas kernels: 868 us -> 781 us
  local copies, waits for them, and re-layouts: 23.6 us -> 14.5 us
    pallas_call x2, Pallas kernels: 868 us -> 781 us  [the longest x1 576 us: mlp_phase(): pl.pallas_call(functools.partial(mlp_kernel, n_chunks), out_shape=tuple((...]
where the time goes in v3:
time: 801 us; the launch traced here: 800 us
  Pallas kernels  781 us (98%)
  local copies, waits for them, and re-layouts  14.5 us (2%)
    pallas_call x1, Pallas kernels, mlp_phase(): pl.pallas_call(functools.partial(mlp_kernel, n_chunks), out_shape=tuple((...  576 us
    pallas_call x1, Pallas kernels, attn_phase(): pl.pallas_call(functools.partial(attn_kernel, n_chunks), out_shape=tuple(...  206 us

profile of v3, /device:TPU:97, one launch (start us, length us, event | category | flops | bytes accessed | tf_op | source)
XLA Modules:
  0.0 799.9 jit_solution(650440479688751652)
XLA Ops:
  0.0 0.7 stack.9
  0.7 0.7 stack.10
  1.4 0.6 maximum_convert_fusion.gains
  2.0 1.9 fusion
  3.9 1.4 pad_maximum_fusion
  5.3 206.0 %attn_phase.1 = (bf16[1024,1792]{1,0:T(8,128)(2,1)}, bf16[128,1792]{1,0:T(8,128)(2,1)}, bf16[3072,1792]{1,0:T(8,128)(2,1)}) custom-call(bf16[4096,1792]{1,0:T(8,128)(2,1)} %x_hbm.3, f32[2,1792]{1,0:T(2,128)} %maximum_convert_fusion.gains, f32[1024,128]{1,0:T(8,128)} %get-tuple-element.16.cos_t, f32[1024,128]{1,0:T(8,128)} %get-tuple-element.17.sin_t, ...), custom_call_target="tpu_custom_call" | custom-call | tf_op jit(solution)/shard_map/attn_phase/pallas_call | solution.py:886
  211.3 575.5 %mlp_phase.1 = (bf16[4096,1792]{1,0:T(8,128)(2,1)}, bf16[3072,1792]{1,0:T(8,128)(2,1)}, bf16[384,1792]{1,0:T(8,128)(2,1)}) custom-call(bf16[4096,1792]{1,0:T(8,128)(2,1)} %x_hbm.3, f32[2,1792]{1,0:T(2,128)} %maximum_convert_fusion.gains, bf16[1024,1792]{1,0:T(8,128)(2,1)} %get-tuple-element.9.me_hbm, bf16[128,1792]{1,0:T(8,128)(2,1)} %get-tuple-element.10.he_hbm, ...), custom_call_target="tpu_custom_call" | custom-call | tf_op jit(solution)/shard_map/mlp_phase/pallas_call | solution.py:508
  786.8 13.1 %copy.12 = bf16[4096,1792]{1,0:T(8,128)(2,1)} copy(bf16[4096,1792]{1,0:T(8,128)(2,1)} %get-tuple-element.12) | data formatting | bytes 29360128
  (2 shorter events, 0.0 us)

commit v4 on v3

--- a/solution.py
+++ b/solution.py
@@ -164,7 +164,25 @@
     def dd_copy():
         return rcopy(DP.at[rows((1 - at.core) * hb, hb, hb)], DR, dds, ddr, at.dev_core)
 
+    def last_copy():
+        return rcopy(DP.at[rows((1 - at.core) * hb, hb, hb)], OR, ods, odr, at.dev_core)
+
+    def down(par):
+        @pl.loop(0, width // dn_w)
+        def _(n):
+            cols = rows(n * dn_w, dn_w, 128)
+            DP[:, cols] = jnp.dot(ACT[par], WD[:, cols], preferred_element_type=F32).astype(BF16)
+
     own_half = at.core * hb
+
+    def core_add(part):
+        @pl.loop(0, hb // 16)
+        def _(i):
+            ri = rows(i * 16, 16, 16)
+            ra = rows(own_half + i * 16, 16, 16)
+            DP[ra, :] = (DP[ra, :].astype(F32) + part[ri, :].astype(F32)).astype(BF16)
+
+        start(x1_copies())
 
     def x1_copies():
         o = own_half + at.xo * xb
@@ -381,15 +399,13 @@
 
         m_step(o_pass)
 
-        @pl.when(has_d)
+        is_last = k == n_chunks + 1
+        has_dd = jnp.logical_and(has_d, k < n_chunks + 1)
+
+        @pl.when(has_dd)
         def _():
             wait(fwd_copies(par))
-
-            @pl.loop(0, width // dn_w)
-            def _(n):
-                cols = rows(n * dn_w, dn_w, 128)
-                DP[:, cols] = jnp.dot(ACT[par], WD[:, cols], preferred_element_type=F32).astype(BF16)
-
+            down(par)
             dd_copy().start()
 
         o_step(o_core)
@@ -417,18 +433,15 @@
         def _():
             m_start(k + 1)
 
-        @pl.when(has_d)
+        @pl.when(has_dd)
         def _():
             dd_copy().wait()
-            step = 16
-
-            @pl.loop(0, hb // step)
-            def _(i):
-                ri = rows(i * step, step, step)
-                ra = rows(own_half + i * step, step, step)
-                DP[ra, :] = (DP[ra, :].astype(F32) + DR[ri, :].astype(F32)).astype(BF16)
-
-            start(x1_copies())
+            core_add(DR)
+
+        @pl.when(is_last)
+        def _():
+            last_copy().wait()
+            core_add(OR)
 
         @pl.when(has_gu)
         def _():
@@ -464,6 +477,12 @@
             YB[r, :] = (H[...].astype(F32) + down).astype(BF16)
             start(xa_copies())
             dy_copy(0).start()
+
+        @pl.when(k == n_chunks)
+        def _():
+            wait(fwd_copies(alt))
+            down(alt)
+            last_copy().start()
 
         @pl.when(has_gu)
         def _():
@@ -528,7 +547,7 @@
 def attn_kernel(n_chunks, x_hbm, gains, cos_t, sin_t, wq_hbm, wk_hbm, wv_hbm, wo_hbm, m_hbm, h_hbm, wp_hbm,
                 WQKV, WO, X, N, QP, R1, R2, QS, KV, O, WP, DR, XR1, XR2, XH, HB, MO, SQ, RC, ST1, ST2,
                 w_sem, x_sem, xh_sem, hb_sem, mo_sem, wp_sem, credit,
-                t1s, t1r, s1s, s1r, s2s, s2r, kvs, kvr, ocs, ocr, ofs, ofr, dds, ddr, x1s, x1r, x2s, x2r, t2s, t2r, xas, xar, xfs, xfr, dms, dmr):
+                t1s, t1r, s1s, s1r, s2s, s2r, kvs, kvr, kfs, kfr, ocs, ocr, ofs, ofr, dds, ddr, x1s, x1r, x2s, x2r, t2s, t2r, xas, xar, xfs, xfr, dms, dmr):
     at = Place()
     tc, width = N.shape
     full_width = width * 4
@@ -580,8 +599,12 @@
         return two([QP.at[s, rows(b * qb, qb, qb)] for b in (at.yp, at.ym)], slots(R2.at[s]), s2s.at[pair(c)], s2r.at[s], at.ys)
 
     def kv_copies(c):
-        own = KV.at[rows(c * tc + at.y * qb, qb, qb)]
-        return [rcopy(own, own, kvs.at[pair(c), i], kvr.at[c, i], dev) for i, dev in enumerate(peers)]
+        own = [KV.at[rows(c * tc + at.y * qb, qb, qb)]] * 2
+        return two(own, own, kvs.at[pair(c)], kvr.at[c], at.ys)
+
+    def kf_copies(c):
+        half = [KV.at[rows(c * tc + r, hq, hq)] for r in (at.ym * qb, at.yp * qb + hq)]
+        return two(half, half, kfs.at[pair(c)], kfr.at[c], at.ys)
 
     def o_copies(c):
         own = [O.at[slot(c), rows(at.y * qb, qb, qb)]] * 2
@@ -717,8 +740,12 @@
         for i in range(heads):
             QS[pair(c), i * qb:(i + 1) * qb, :] = turned(i)
 
+    def st_kvfwd(c):
+        wait(kv_copies(c))
+        start(kf_copies(c))
+
     def st_attend(c):
-        wait(kv_copies(c))
+        wait(kf_copies(c))
         q = QS[pair(c)]
         scale = head ** -0.5 * 1.4426950408889634
 
@@ -748,6 +775,8 @@
         out = (acc / total).astype(BF16)
         for i in range(heads):
             O[slot(c), rows(at.y * qb, qb, qb), i * head:(i + 1) * head] = out[i * qb:(i + 1) * qb, :]
+
+    def st_osend(c):
         start(o_copies(c))
 
     def st_ofwd(c):
@@ -848,8 +877,9 @@
         for i in range(4):
             dm_wait_recv(c, i)
 
-    bodies = (st_sumsq, st_qkv, st_add1, st_rope, st_attend, st_ofwd, st_oproj, st_x1, st_x2, st_h, st_m, st_xf, st_dm, st_end)
-    n_iter = max(n_chunks + 7, EARLY + len(bodies) - 1)
+    steps = ((0, st_sumsq), (1, st_qkv), (2, st_add1), (3, st_rope), (4, st_attend), (3, st_kvfwd), (4, st_osend), (5, st_ofwd), (6, st_oproj),
+             (7, st_x1), (8, st_x2), (9, st_h), (10, st_m), (11, st_xf), (12, st_dm), (13, st_end))
+    n_iter = max(n_chunks + 7, EARLY + 13)
 
     @pl.loop(0, n_iter)
     def _(k):
@@ -857,9 +887,9 @@
         def _():
             at.take_credit(credit)
 
-        for s, body in enumerate(bodies):
+        for s, body in steps:
             stage(k, s, body)
-            if s == 1:
+            if body is st_qkv:
                 @pl.when(k + 1 < n_chunks)
                 def _():
                     x_copy(k + 1).start()
@@ -894,13 +924,40 @@
             vm(4, chunk, width), vm(4, hb, width), vm(4, 2, xb // 2, width), vm(4, 2, xb, width), vm(2, xb, width), vm(4, xb, width), vm(4, xb, width),
             vf(chunk, 128), vf(chunk, 128), vf(n_chunks, 4, 8, 128), vf(n_chunks, 4, 8, 128),
             sem((heads + 3,)), S2, S2, S2, S2, S2, pltpu.SemaphoreType.REGULAR((5,)),
-            sem((2, 3)), sem((n_chunks, 3)), P2, sem((4, 2)), P2, sem((4, 2)), sem((2, 3)), sem((n_chunks, 3)),
+            sem((2, 3)), sem((n_chunks, 3)), P2, sem((4, 2)), P2, sem((4, 2)), P2, sem((n_chunks, 2)), P2, sem((n_chunks, 2)),
             P2, sem((4, 2)), P2, sem((4, 2)), S2, sem((4,)), P2, sem((4, 2)), P2, sem((4, 2)),
             sem((2, 3)), sem((n_chunks, 3)), P2, sem((n_chunks, 2)), P2, sem((n_chunks, 2)), sem((2, 4)), sem((n_chunks, 4)),
         ],
         compiler_params=pltpu.CompilerParams(collective_id=2, has_side_effects=True, vmem_limit_bytes=67043328),
         name="attn_phase",
     )(x_in, gains, cos_t, sin_t, w_q, w_k, w_v, w_o)
+
+
+def copy_kernel(src, dst, buf, in_sem, out_sem):
+    n, part = buf.shape[:2]
+    ins = [pltpu.make_async_copy(src.at[pl.ds(i * part, part)], buf.at[i], in_sem.at[i]) for i in range(n)]
+    outs = [pltpu.make_async_copy(buf.at[i], dst.at[pl.ds(i * part, part)], out_sem.at[i]) for i in range(n)]
+    start(ins)
+    for i in range(n):
+        ins[i].wait()
+        outs[i].start()
+    for c in outs:
+        c.wait()
+
+
+def copy_out(y):
+    tokens, width = y.shape
+    n = 16
+    hbm = pl.BlockSpec(memory_space=pl.ANY)
+    return pl.pallas_call(
+        copy_kernel,
+        out_shape=jax.ShapeDtypeStruct(y.shape, y.dtype),
+        in_specs=[hbm],
+        out_specs=hbm,
+        scratch_shapes=[pltpu.VMEM((n, tokens // n, width), y.dtype), pltpu.SemaphoreType.DMA((n,)), pltpu.SemaphoreType.DMA((n,))],
+        compiler_params=pltpu.CompilerParams(vmem_limit_bytes=67043328),
+        name="copy_out",
+    )(y)
 
 
 def solution(mesh, chunk=CHUNK):
@@ -921,7 +978,7 @@
         gains = jnp.stack([gain_attn, gain_mlp]).astype(F32)
         m_early, h_early, o_part = attn_phase(
             x_in, gains, cos_t, sin_t, w_q.transpose(1, 0, 2), w_k.reshape(width, -1), w_v.reshape(width, -1), w_o.reshape(-1, width), chunk)
-        return mlp_phase(x_in, gains, m_early, h_early, o_part, w_gate, w_up, w_down, chunk)
+        return copy_out(mlp_phase(x_in, gains, m_early, h_early, o_part, w_gate, w_up, w_down, chunk))
 
     in_specs = (P("dp", "my"), P("my"), P("my", "mx", None), P("my", "mx", None), P("my", "mx", None), P("mx", None, "my"), P("my"), P("my", "mx"), P("my", "mx"), P("mx", "my"))
     return jax.shard_map(local_layer, mesh=mesh, in_specs=in_specs, out_specs=P("dp", "my"), check_vma=False)

time: 801 us -> 813 us (1.015)
  Pallas kernels: 781 us -> 807 us
  local copies, waits for them, and re-layouts: 14.5 us -> 1.39 us
    pallas_call x1, Pallas kernels: 206 us -> 229 us  [attn_phase(): pl.pallas_call(functools.partial(attn_kernel, n_chunks), out_shape=tuple(...]
    unnamed x1 -> x0, local copies, waits for them, and re-layouts: 13.1 us -> none
    pallas_call x0 -> x1, Pallas kernels: none -> 10.9 us  [copy_out(): pl.pallas_call(copy_kernel, out_shape=jax.ShapeDtypeStruct(y.shape, y.dty...]
    pallas_call x1, Pallas kernels: 576 us -> 567 us  [mlp_phase(): pl.pallas_call(functools.partial(mlp_kernel, n_chunks), out_shape=tuple((...]
where the time goes in v4:
time: 813 us
  Pallas kernels  807 us (99%)
    pallas_call x1, Pallas kernels, mlp_phase(): pl.pallas_call(functools.partial(mlp_kernel, n_chunks), out_shape=tuple((...  567 us
    pallas_call x1, Pallas kernels, attn_phase(): pl.pallas_call(functools.partial(attn_kernel, n_chunks), out_shape=tuple(...  229 us

profile of v4, /device:TPU:97, one launch (start us, length us, event | category | flops | bytes accessed | tf_op | source)
XLA Modules:
  0.0 812.5 jit_solution(9038033326292494558)
XLA Ops:
  0.0 0.7 stack.9
  0.7 0.7 stack.10
  1.4 0.6 maximum_convert_fusion.gains
  2.0 1.9 fusion
  3.9 1.4 pad_maximum_fusion
  5.3 229.0 %attn_phase.1 = (bf16[1024,1792]{1,0:T(8,128)(2,1)}, bf16[128,1792]{1,0:T(8,128)(2,1)}, bf16[3072,1792]{1,0:T(8,128)(2,1)}) custom-call(bf16[4096,1792]{1,0:T(8,128)(2,1)} %x_hbm.3, f32[2,1792]{1,0:T(2,128)} %maximum_convert_fusion.gains, f32[1024,128]{1,0:T(8,128)} %get-tuple-element.16.cos_t, f32[1024,128]{1,0:T(8,128)} %get-tuple-element.17.sin_t, ...), custom_call_target="tpu_custom_call" | custom-call | tf_op jit(solution)/shard_map/attn_phase/pallas_call | solution.py:916
  234.3 567.2 %mlp_phase.1 = (bf16[4096,1792]{1,0:T(8,128)(2,1)}, bf16[3072,1792]{1,0:T(8,128)(2,1)}, bf16[384,1792]{1,0:T(8,128)(2,1)}) custom-call(bf16[4096,1792]{1,0:T(8,128)(2,1)} %x_hbm.3, f32[2,1792]{1,0:T(2,128)} %maximum_convert_fusion.gains, bf16[1024,1792]{1,0:T(8,128)(2,1)} %get-tuple-element.9.me_hbm, bf16[128,1792]{1,0:T(8,128)(2,1)} %get-tuple-element.10.he_hbm, ...), custom_call_target="tpu_custom_call" | custom-call | tf_op jit(solution)/shard_map/mlp_phase/pallas_call | solution.py:527
  801.4 10.9 %copy_out.1 = bf16[4096,1792]{1,0:T(8,128)(2,1)} custom-call(bf16[4096,1792]{1,0:T(8,128)(2,1)} %get-tuple-element.12.src), custom_call_target="tpu_custom_call" | custom-call | tf_op jit(solution)/shard_map/copy_out/pallas_call | solution.py:952
  (2 shorter events, 0.0 us)

commit v5 on v4

--- a/solution.py
+++ b/solution.py
@@ -223,8 +223,8 @@
         def _():
             pltpu.make_async_copy(hl_hbm.at[rows((c - EARLY) * xb, xb, xb)], H, h_sem).start()
 
-    def y_copy(c):
-        return pltpu.make_async_copy(YB, y_hbm.at[rows(c * tc, tc, tc)], y_sem)
+    def y_copy(c, core):
+        return pltpu.make_async_copy(YB.at[rows(core * hb, hb, hb)], y_hbm.at[rows(c * tc + core * hb, hb, hb)], y_sem.at[core])
 
     my_rows = own_half + at.x * xb
     peers = at.ys + (at.dev_yo,)
@@ -503,11 +503,13 @@
         def _():
             wait(xf_copies())
             dy_copy(3).start()
+            y_copy(k - 2, at.core).start()
             for i in range(4):
                 dy_copy(i).wait_send()
                 dy_wait_recv(i)
-            y_copy(k - 2).start()
-            y_copy(k - 2).wait()
+            y_copy(k - 2, 1 - at.core).start()
+            for i in range(2):
+                y_copy(k - 2, i).wait()
 
         @pl.when(k < n_chunks + 1)
         def _():
@@ -535,7 +537,7 @@
             vm(2, xb // 2, width), vm(2, xb, width), vm(chunk, width), vm(xb, width),
             vm(hb, width), vm(hb, width), vm(2, xb // 2, width), vm(2, xb, width), vm(xb, width), vm(xb, width), vm(xb, width),
             pltpu.VMEM((n_chunks, 4, 8, 128), F32),
-            sem((11,)), sem, sem, sem, sem((4,)), sem, sem, sem((4, 2)), sem((4, 2)), sem((3,)), sem((n_chunks, 3)), sem((4,)), sem((4,)), pltpu.SemaphoreType.REGULAR((5,)),
+            sem((11,)), sem, sem, S2, sem((4,)), sem, sem, sem((4, 2)), sem((4, 2)), sem((3,)), sem((n_chunks, 3)), sem((4,)), sem((4,)), pltpu.SemaphoreType.REGULAR((5,)),
             S2, S2, P2, P2, S2, S2, P2, P2,
             sem, sem, S2, S2, S2, S2, S2, S2, S2, S2, sem((4,)), sem((4,)),
         ],
@@ -661,7 +663,7 @@
     def stage(k, s, body):
         c = k - s
 
-        @pl.when(jnp.logical_and(c >= 0, c < (EARLY if s >= 8 else n_chunks)))
+        @pl.when(jnp.logical_and(c >= 0, c < (EARLY if body in early_chunks else n_chunks)))
         def _():
             body(c)
 
@@ -738,7 +740,7 @@
         KV[kv_rows, head:2 * head] = piece(heads + 1)
         start(kv_copies(c))
         for i in range(heads):
-            QS[pair(c), i * qb:(i + 1) * qb, :] = turned(i)
+            QS[slot(c), i * qb:(i + 1) * qb, :] = turned(i)
 
     def st_kvfwd(c):
         wait(kv_copies(c))
@@ -746,7 +748,7 @@
 
     def st_attend(c):
         wait(kf_copies(c))
-        q = QS[pair(c)]
+        q = QS[slot(c)]
         scale = head ** -0.5 * 1.4426950408889634
 
         def scores(j):
@@ -775,8 +777,6 @@
         out = (acc / total).astype(BF16)
         for i in range(heads):
             O[slot(c), rows(at.y * qb, qb, qb), i * head:(i + 1) * head] = out[i * qb:(i + 1) * qb, :]
-
-    def st_osend(c):
         start(o_copies(c))
 
     def st_ofwd(c):
@@ -877,9 +877,10 @@
         for i in range(4):
             dm_wait_recv(c, i)
 
-    steps = ((0, st_sumsq), (1, st_qkv), (2, st_add1), (3, st_rope), (4, st_attend), (3, st_kvfwd), (4, st_osend), (5, st_ofwd), (6, st_oproj),
-             (7, st_x1), (8, st_x2), (9, st_h), (10, st_m), (11, st_xf), (12, st_dm), (13, st_end))
-    n_iter = max(n_chunks + 7, EARLY + 13)
+    all_chunks = (st_sumsq, st_qkv, st_add1, st_rope, st_kvfwd, st_attend, st_ofwd, st_oproj, st_x1)
+    early_chunks = (st_x2, st_h, st_m, st_xf, st_dm, st_end)
+    steps = all_chunks + early_chunks
+    n_iter = max(n_chunks + len(all_chunks), EARLY + len(steps)) - 1
 
     @pl.loop(0, n_iter)
     def _(k):
@@ -887,7 +888,7 @@
         def _():
             at.take_credit(credit)
 
-        for s, body in steps:
+        for s, body in enumerate(steps):
             stage(k, s, body)
             if body is st_qkv:
                 @pl.when(k + 1 < n_chunks)
@@ -920,7 +921,7 @@
         out_specs=(hbm, hbm, hbm),
         scratch_shapes=[
             vm(width, qkv_w), vm(q_w, width), vm(2, chunk, width), vm(chunk, width), vm(4, chunk, qkv_w),
-            vm(4, 2, qb // 2, qkv_w), vm(4, 2, qb, qkv_w), vm(2, heads * qb, 128), vm(tokens, 256), vm(4, chunk, q_w),
+            vm(4, 2, qb // 2, qkv_w), vm(4, 2, qb, qkv_w), vm(4, heads * qb, 128), vm(tokens, 256), vm(4, chunk, q_w),
             vm(4, chunk, width), vm(4, hb, width), vm(4, 2, xb // 2, width), vm(4, 2, xb, width), vm(2, xb, width), vm(4, xb, width), vm(4, xb, width),
             vf(chunk, 128), vf(chunk, 128), vf(n_chunks, 4, 8, 128), vf(n_chunks, 4, 8, 128),
             sem((heads + 3,)), S2, S2, S2, S2, S2, pltpu.SemaphoreType.REGULAR((5,)),

time: 813 us -> 788 us (0.969)
  Pallas kernels: 807 us -> 782 us
    pallas_call x1, Pallas kernels: 229 us -> 205 us  [attn_phase(): pl.pallas_call(functools.partial(attn_kernel, n_chunks), out_shape=tuple(...]
where the time goes in v5:
time: 788 us
  Pallas kernels  782 us (99%)
    pallas_call x1, Pallas kernels, mlp_phase(): pl.pallas_call(functools.partial(mlp_kernel, n_chunks), out_shape=tuple((...  567 us
    pallas_call x1, Pallas kernels, attn_phase(): pl.pallas_call(functools.partial(attn_kernel, n_chunks), out_shape=tuple(...  205 us

profile of v5, /device:TPU:97, one launch (start us, length us, event | category | flops | bytes accessed | tf_op | source)
XLA Modules:
  0.0 787.6 jit_solution(3966294413703998214)
XLA Ops:
  0.0 0.7 stack.9
  0.7 0.7 stack.10
  1.4 0.6 maximum_convert_fusion.gains
  2.0 1.9 fusion
  3.9 1.4 pad_maximum_fusion
  5.3 204.7 %attn_phase.1 = (bf16[1024,1792]{1,0:T(8,128)(2,1)}, bf16[128,1792]{1,0:T(8,128)(2,1)}, bf16[3072,1792]{1,0:T(8,128)(2,1)}) custom-call(bf16[4096,1792]{1,0:T(8,128)(2,1)} %x_hbm.3, f32[2,1792]{1,0:T(2,128)} %maximum_convert_fusion.gains, f32[1024,128]{1,0:T(8,128)} %get-tuple-element.16.cos_t, f32[1024,128]{1,0:T(8,128)} %get-tuple-element.17.sin_t, ...), custom_call_target="tpu_custom_call" | custom-call | tf_op jit(solution)/shard_map/attn_phase/pallas_call | solution.py:917
  210.0 566.5 %mlp_phase.1 = (bf16[4096,1792]{1,0:T(8,128)(2,1)}, bf16[3072,1792]{1,0:T(8,128)(2,1)}, bf16[384,1792]{1,0:T(8,128)(2,1)}) custom-call(bf16[4096,1792]{1,0:T(8,128)(2,1)} %x_hbm.3, f32[2,1792]{1,0:T(2,128)} %maximum_convert_fusion.gains, bf16[1024,1792]{1,0:T(8,128)(2,1)} %get-tuple-element.9.me_hbm, bf16[128,1792]{1,0:T(8,128)(2,1)} %get-tuple-element.10.he_hbm, ...), custom_call_target="tpu_custom_call" | custom-call | tf_op jit(solution)/shard_map/mlp_phase/pallas_call | solution.py:529
  776.5 10.9 %copy_out.1 = bf16[4096,1792]{1,0:T(8,128)(2,1)} custom-call(bf16[4096,1792]{1,0:T(8,128)(2,1)} %get-tuple-element.12.src), custom_call_target="tpu_custom_call" | custom-call | tf_op jit(solution)/shard_map/copy_out/pallas_call | solution.py:953
  (2 shorter events, 0.0 us)

commit v6 on v5

--- a/solution.py
+++ b/solution.py
@@ -134,9 +134,9 @@
 
     wd_copy = pltpu.make_async_copy(wd_hbm, WD, w_sem.at[2 * gu_tiles])
     pltpu.make_async_copy(me_hbm.at[pl.ds(0, tc)], M, m_sem).start()
-    for n in range(gu_tiles):
+    ahead = 2
+    for n in range(ahead):
         start(gu_copies(n))
-    wd_copy.start()
     at.entry(extra=(at.dev_yo,))
 
     def gu_part(par, lo, hi):
@@ -338,6 +338,10 @@
         @pl.loop(0, gu_tiles)
         def _(n):
             if i == 0:
+                @pl.when(n + ahead < gu_tiles)
+                def _():
+                    start(gu_copies(n + ahead))
+
                 wait(gu_copies(n))
             g_cols = rows(n * gu_w, gu_w, 128)
             PP[0, br, g_cols] = jnp.dot(M[br, :], WG[:, g_cols], preferred_element_type=F32).astype(BF16)
@@ -345,6 +349,7 @@
 
         if i == 0:
             start(s1_copies(0))
+            wd_copy.start()
     wd_copy.wait()
 
     @pl.loop(0, n_chunks + 2)
@@ -972,10 +977,10 @@
         positions = (row // qb) * chunk + lax.axis_index("my") * qb + row % qb
         half = head // 2
         inv_freq = ROPE_BASE ** (-jnp.arange(half, dtype=F32) / half)
+        inv_freq = jnp.concatenate([inv_freq, inv_freq])
         angles = positions.astype(F32)[:, None] * inv_freq[None, :]
-        cos_h, sin_h = jnp.cos(angles), jnp.sin(angles)
-        cos_t = jnp.concatenate([cos_h, cos_h], axis=-1)
-        sin_t = jnp.concatenate([-sin_h, sin_h], axis=-1)
+        cos_t = jnp.cos(angles)
+        sin_t = jnp.sin(angles) * jnp.where(jnp.arange(head) < half, -1.0, 1.0)
         gains = jnp.stack([gain_attn, gain_mlp]).astype(F32)
         m_early, h_early, o_part = attn_phase(
             x_in, gains, cos_t, sin_t, w_q.transpose(1, 0, 2), w_k.reshape(width, -1), w_v.reshape(width, -1), w_o.reshape(-1, width), chunk)

time: 788 us -> 786 us (level)
  no operation moved by 1% of the time
where the time goes in v6:
time: 786 us
  Pallas kernels  780 us (99%)
    pallas_call x1, Pallas kernels, mlp_phase(): pl.pallas_call(functools.partial(mlp_kernel, n_chunks), out_shape=tuple((...  565 us
    pallas_call x1, Pallas kernels, attn_phase(): pl.pallas_call(functools.partial(attn_kernel, n_chunks), out_shape=tuple(...  205 us

profile of v6, /device:TPU:97, one launch (start us, length us, event | category | flops | bytes accessed | tf_op | source)
XLA Modules:
  0.0 785.6 jit_solution(9372146127590593024)
XLA Ops:
  0.0 0.1 compare_select_fusion
  0.1 0.7 stack.9
  0.8 0.7 stack.10
  1.5 0.6 maximum_convert_fusion.gains
  2.1 3.0 fusion
  5.1 204.7 %attn_phase.1 = (bf16[1024,1792]{1,0:T(8,128)(2,1)}, bf16[128,1792]{1,0:T(8,128)(2,1)}, bf16[3072,1792]{1,0:T(8,128)(2,1)}) custom-call(bf16[4096,1792]{1,0:T(8,128)(2,1)} %x_hbm.3, f32[2,1792]{1,0:T(2,128)} %maximum_convert_fusion.gains, f32[1024,128]{1,0:T(8,128)} %get-tuple-element.14.cos_t, f32[1024,128]{1,0:T(8,128)} %get-tuple-element.13.sin_t, ...), custom_call_target="tpu_custom_call" | custom-call | tf_op jit(solution)/shard_map/attn_phase/pallas_call | solution.py:922
  209.8 564.7 %mlp_phase.1 = (bf16[4096,1792]{1,0:T(8,128)(2,1)}, bf16[3072,1792]{1,0:T(8,128)(2,1)}, bf16[384,1792]{1,0:T(8,128)(2,1)}) custom-call(bf16[4096,1792]{1,0:T(8,128)(2,1)} %x_hbm.3, f32[2,1792]{1,0:T(2,128)} %maximum_convert_fusion.gains, bf16[1024,1792]{1,0:T(8,128)(2,1)} %get-tuple-element.9.me_hbm, bf16[128,1792]{1,0:T(8,128)(2,1)} %get-tuple-element.10.he_hbm, ...), custom_call_target="tpu_custom_call" | custom-call | tf_op jit(solution)/shard_map/mlp_phase/pallas_call | solution.py:534
  774.5 10.9 %copy_out.1 = bf16[4096,1792]{1,0:T(8,128)(2,1)} custom-call(bf16[4096,1792]{1,0:T(8,128)(2,1)} %get-tuple-element.12.src), custom_call_target="tpu_custom_call" | custom-call | tf_op jit(solution)/shard_map/copy_out/pallas_call | solution.py:958
  (2 shorter events, 0.0 us)
